TPU v7x, 32 devices: a whole 2x2x4 slice. The times are simulated.
32 devices in a mesh: node: 8 (over y, x, core), grp: 4 (over z).
Axes of the slice: x: 2, y: 2, z: 4, core: 2. Of those that a mesh axis runs over, the one named last changes fastest.
Arguments:
- tokens: bfloat16 [12288, 1792], P(('node', 'grp')), may hold values from -6 to 6
- cotangent: bfloat16 [12288, 1792], P(('node', 'grp')), may hold values from -6 to 6
- gate_weight: bfloat16 [1792, 1024], P('node'), may hold values from -0.125 to 0.125
- up_weight: bfloat16 [1792, 1024], P('node'), may hold values from -0.125 to 0.125
- down_weight_t: bfloat16 [1792, 1024], P('node'), may hold values from -0.125 to 0.125
- error_memory: bfloat16 [4, 1792, 3072], P('grp', 'node'), may hold values from -4 to 4
- q_init: float32 [3, 1024, 32], replicated, may hold values from -6 to 6
Outputs:
- token_grad: bfloat16 [12288, 1792], P(('node', 'grp'))
- new_error: bfloat16 [4, 1792, 3072], P('grp', 'node')
- p_hat: float32 [3, 1792, 32], P(None, 'node')
- q_new: float32 [3, 1024, 32], replicated
All inputs are finite; a program needn't handle non-finite values.
Results may differ from a plain program's by a relative error of at most 0.012.
Values may be sent and summed in bfloat16 or wider, within the bound.
A program may use at most 192 MiB of HBM per device.

v0:
```python
import functools
import math

import jax
import jax.numpy as jnp
from jax import lax
from jax.experimental import pallas as pl
from jax.experimental.pallas import tpu as pltpu
from jax.sharding import PartitionSpec as P

MESH = pl.DeviceIdType.MESH
F32, BF16 = jnp.float32, jnp.bfloat16
HIGHEST = lax.Precision.HIGHEST
LANES = 128


def gelu_parts(value):
    coeff = math.sqrt(2.0 / math.pi)
    square = value * value
    tanh_value = jnp.tanh(coeff * (value + 0.044715 * square * value))
    activation = 0.5 * value * (1.0 + tanh_value)
    slope = 0.5 * (1.0 + tanh_value) + 0.5 * value * (1.0 - tanh_value * tanh_value) * coeff * (
        1.0 + 3.0 * 0.044715 * square
    )
    return activation, slope


def dot(a, b, precision=None):
    return jnp.dot(a, b, preferred_element_type=F32, precision=precision)


def dot_nt(a, b, precision=None):
    return lax.dot_general(
        a, b, (((1,), (1,)), ((), ())), preferred_element_type=F32, precision=precision
    )


def subsets(items):
    found = [()]
    for item in items:
        found += [s + (item,) for s in found]
    return found


def kernel(
    n, g, rank, n_recv,
    tok, cot, w_gate, w_up, w_down, err, q_pad,
    tok_grad, new_err, p_out, q_out,
    full, tok_t, cot_t, act, ups, hid, d_up, d_gate, grads, *rest
):
    recv_bufs = rest[:n_recv]
    (merged, power, hat, block_diag, q_t, pw_all, gram_all, q_part, q_rs, q_grp, q_all,
     send_sems, recv_sems, local_sems) = rest[n_recv:]
    me, grp = lax.axis_index("node"), lax.axis_index("grp")
    rows, hidden = w_gate.shape
    depth = tok.shape[1]
    half = hidden // 2
    bits = n.bit_length() - 1
    tile = 256
    used = 3 * rank
    weights = (w_gate, w_up, w_down)

    barrier = pltpu.get_barrier_semaphore()
    for d in range(1, n):
        pl.semaphore_signal(barrier, inc=1, device_id=(lax.rem(me + d, n), grp), device_id_type=MESH)
    for d in range(1, g):
        pl.semaphore_signal(barrier, inc=1, device_id=(me, lax.rem(grp + d, g)), device_id_type=MESH)

    flip = [(1 << b) * (1 - 2 * lax.rem(me // (1 << b), 2)) for b in range(bits)]
    offset = lambda mask: sum((flip[b] for b in mask), 0)
    outer = list(range(1, bits))
    orders = [outer + [0], outer[::-1] + [0]]
    rs_orders = [[0] + outer, [0] + outer[::-1]]
    cols = [pl.ds(h * half, half) for h in range(2)]
    block = lambda index: pl.ds(pl.multiple_of(index * rows, rows), rows)

    count = [0]
    started = []

    def send(src, dst, node, group):
        copy = pltpu.make_async_remote_copy(
            src_ref=src, dst_ref=dst,
            send_sem=send_sems.at[count[0]], recv_sem=recv_sems.at[count[0]],
            device_id=(node, group), device_id_type=MESH,
        )
        count[0] += 1
        started.append(copy)
        copy.start()
        return copy

    locals_ = []
    for w in range(3):
        copy = pltpu.make_async_copy(weights[w], full.at[w, block(me)], local_sems.at[w])
        copy.start()
        locals_.append(copy)
    pl.semaphore_wait(barrier, n - 1 + g - 1)

    gathers = {}

    def gather_send(w, t, h, mask):
        at = (w, block(me + offset(mask)), cols[h])
        src = full.at[at] if mask else weights[w].at[:, cols[h]]
        copy = send(src, full.at[at], me + flip[orders[h][t]], grp)
        gathers.setdefault((w, t, h), []).append(copy)

    def gather_start(w, t):
        for h in range(2):
            held = subsets(orders[h][:t])
            if t < bits - 1:
                for mask in held:
                    gather_send(w, t, h, mask)
            for mask in held:
                if t == 0 or orders[h][t - 1] in mask:
                    gather_send(w, bits - 1, h, mask)

    def gather_finish(w, t):
        for h in range(2):
            for copy in gathers[w, t, h]:
                copy.wait_recv()

    for w in range(2):
        gather_start(w, 0)

    @pl.loop(0, depth // tile)
    def _(i):
        at = pl.ds(pl.multiple_of(i * tile, tile), tile)
        tok_t[at, :] = tok[:, at].T
        cot_t[at, :] = cot[:, at].T

    merged[...] = jnp.zeros_like(merged)
    power[...] = jnp.zeros_like(power)
    hat[...] = jnp.zeros_like(hat)
    block_diag[...] = jnp.zeros_like(block_diag)
    q_t[...] = jnp.zeros_like(q_t)
    for copy in locals_:
        copy.wait()

    for t in range(1, bits - 1):
        for w in range(2):
            gather_finish(w, t - 1)
            gather_start(w, t)
    gather_start(2, 0)
    gather_finish(0, bits - 2)
    gather_start(0, bits - 1)
    gather_finish(0, bits - 1)

    @pl.loop(0, hidden // tile)
    def _(j):
        at = pl.ds(pl.multiple_of(j * tile, tile), tile)
        act[:, at] = dot(tok[...], full[0, :, at])

    gather_finish(1, bits - 2)
    gather_start(1, bits - 1)
    gather_finish(1, bits - 1)

    def up_part(first, last):
        @pl.loop(first, last)
        def _(j):
            at = pl.ds(pl.multiple_of(j * tile, tile), tile)
            up_pre = dot(tok[...], full[1, :, at])
            activation, slope = gelu_parts(act[:, at])
            act[:, at] = activation
            ups[:, at] = up_pre * slope
            hid[:, at] = (activation * up_pre).astype(BF16)

    tiles = hidden // tile
    up_part(0, tiles // 2)
    for t in range(1, bits - 1):
        gather_finish(2, t - 1)
        gather_start(2, t)
    up_part(tiles // 2, tiles)

    reduces = {}

    steps = depth // tile

    def partial_grad(m, left, right, first=0, last=steps):
        @pl.loop(first, last)
        def _(i):
            at = pl.ds(pl.multiple_of(i * tile, tile), tile)
            grads[m, at, :] = dot(left[at, :], right[...]).astype(BF16)

    def reduce_start(m, t):
        for h in range(2):
            bit = rs_orders[h][t]
            reduces[m, t, h] = []
            for slot, mask in enumerate(subsets(rs_orders[h][t + 1:])):
                src = grads.at[m, block(me + flip[bit] + offset(mask)), cols[h]]
                dst = recv_bufs[t].at[m, slot, :, cols[h]]
                reduces[m, t, h].append(send(src, dst, me + flip[bit], grp))

    def reduce_add(m, t):
        for h in range(2):
            for slot, mask in enumerate(subsets(rs_orders[h][t + 1:])):
                reduces[m, t, h][slot].wait_recv()
                at = block(me + offset(mask))
                total = (
                    grads[m, at, cols[h]].astype(F32) + recv_bufs[t][m, slot, :, cols[h]].astype(F32)
                )
                if t < bits - 1:
                    grads[m, at, cols[h]] = total.astype(BF16)
                else:
                    scale = 1.0 / math.sqrt(tok.shape[0] * n)
                    memory = err[0, :, pl.ds(m * hidden + h * half, half)].astype(F32)
                    merged[m, 0:rows, cols[h]] = total * scale + memory

    def advance(m, t):
        reduce_add(m, t - 1)
        reduce_start(m, t)

    partial_grad(2, cot_t, hid)
    reduce_start(2, 0)
    gather_finish(2, bits - 2)
    gather_start(2, bits - 1)
    advance(2, 1)
    gather_finish(2, bits - 1)

    @pl.loop(0, hidden // tile)
    def _(j):
        at = pl.ds(pl.multiple_of(j * tile, tile), tile)
        back = dot(cot[...], full[2, :, at])
        d_up[:, at] = (back * act[:, at]).astype(BF16)
        d_gate[:, at] = (back * ups[:, at]).astype(BF16)

    partial_grad(0, tok_t, d_gate)
    reduce_start(0, 0)
    advance(2, 2)
    partial_grad(1, tok_t, d_up, 0, steps // 2)
    advance(0, 1)
    partial_grad(1, tok_t, d_up, steps // 2, steps)
    reduce_start(1, 0)

    def token_part(first, last):
        @pl.loop(first, last)
        def _(i):
            at = pl.ds(pl.multiple_of(i * tile, tile), tile)
            tok_grad[:, at] = (
                dot_nt(d_gate[...], full[0, at, :]) + dot_nt(d_up[...], full[1, at, :])
            ).astype(BF16)

    token_part(0, steps // 3)
    advance(1, 1)
    token_part(steps // 3, 2 * steps // 3)
    advance(0, 2)
    token_part(2 * steps // 3, steps)
    advance(1, 2)
    for t in range(3, bits):
        for m in (2, 0, 1):
            advance(m, t)
    total = jnp.zeros((rows, LANES), F32)
    for m in (2, 0, 1):
        reduce_add(m, bits - 1)
        total += dot(merged[m, 0:rows, :], q_pad[m], HIGHEST)

    pw_all[grp] = total.astype(BF16)
    copies = [
        send(pw_all.at[grp], pw_all.at[grp], me, lax.rem(grp + d, g)) for d in range(1, g)
    ]
    for copy in copies:
        copy.wait_recv()
    total = pw_all[0].astype(F32)
    for k in range(1, g):
        total += pw_all[k].astype(F32)
    power[0:rows, :] = total * (1.0 / g)

    lane = lax.broadcasted_iota(jnp.int32, (rank, LANES), 1)
    row = lax.broadcasted_iota(jnp.int32, (rank, LANES), 0)
    padded = power[...]
    gram = dot(padded.T, padded, HIGHEST)
    picked = gram[0:rank]
    for m in range(1, 3):
        picked = jnp.where(lane >= m * rank, gram[m * rank:(m + 1) * rank], picked)
    gram_all[me] = picked
    copies = [
        send(gram_all.at[me], gram_all.at[me], lax.rem(me + d, n), grp) for d in range(1, n)
    ]
    for copy in copies:
        copy.wait_recv()
    picked = gram_all[0]
    for k in range(1, n):
        picked += gram_all[k]

    work = []
    for m in range(3):
        rolled = picked if m == 0 else pltpu.roll(picked, LANES - m * rank, 1)
        unit = jnp.where(lane == row + rank, 1.0, 0.0).astype(F32)
        work.append(jnp.where(lane < rank, rolled, unit))
    for j in range(rank):
        for m in range(3):
            a = work[m]
            inverse = 1.0 / jnp.sqrt(a[j:j + 1, j:j + 1])
            pivot_row = a[j:j + 1, :] * inverse
            column = a[:, j:j + 1] * inverse
            work[m] = jnp.where(row > j, a - column * pivot_row, jnp.where(row == j, pivot_row, a))
    for m in range(3):
        shift = ((m - 1) * rank) % LANES
        moved = work[m] if shift == 0 else pltpu.roll(work[m], shift, 1)
        inside = (lane >= m * rank) & (lane < (m + 1) * rank)
        block_diag[m * rank:(m + 1) * rank, :] = jnp.where(inside, moved, 0.0)
    hat[0:rows, :] = dot_nt(power[0:rows, :], block_diag[...], HIGHEST)
    p_out[...] = hat[0:rows, :]

    hat_t = hat[...].T
    c_blocks = min(n, hidden // LANES)
    r_blocks = n // c_blocks
    c_size, r_size = hidden // c_blocks, used // r_blocks
    for m in range(3):
        q_t[m * rank:(m + 1) * rank, :] = dot(hat_t[m * rank:(m + 1) * rank], merged[m], HIGHEST)
    spots = [
        (slice(c // c_blocks * r_size, (c // c_blocks + 1) * r_size),
         slice(c % c_blocks * c_size, (c % c_blocks + 1) * c_size))
        for c in range(n)
    ]
    for c in range(n):
        q_part[c] = q_t[spots[c]].astype(BF16)
    q_rs[me] = q_part[me]
    copies = []
    for d in range(1, n):
        to = lax.rem(me + d, n)
        copies.append(send(q_part.at[to], q_rs.at[me], to, grp))
    for copy in copies:
        copy.wait_recv()
    total = q_rs[0].astype(F32)
    for k in range(1, n):
        total += q_rs[k].astype(F32)
    q_grp[grp] = total.astype(BF16)
    copies = [send(q_grp.at[grp], q_grp.at[grp], me, lax.rem(grp + d, g)) for d in range(1, g)]
    for copy in copies:
        copy.wait_recv()
    total = q_grp[0].astype(F32)
    for k in range(1, g):
        total += q_grp[k].astype(F32)
    q_all[me] = (total * (1.0 / g)).astype(BF16)
    copies = [send(q_all.at[me], q_all.at[me], lax.rem(me + d, n), grp) for d in range(1, n)]
    for copy in copies:
        copy.wait_recv()
    for c in range(n):
        q_t[spots[c]] = q_all[c].astype(F32)
    q_out[...] = q_t[0:used, :]

    wide = lax.broadcasted_iota(jnp.int32, (rows, LANES), 1)
    for m in range(3):
        own = jnp.where((wide >= m * rank) & (wide < (m + 1) * rank), hat[0:rows, :], 0.0)
        for h in range(2):
            rebuilt = dot(own, q_t[:, cols[h]], HIGHEST)
            new_err[0, :, pl.ds(m * hidden + h * half, half)] = (
                merged[m, 0:rows, cols[h]] - rebuilt
            ).astype(BF16)
    for copy in started:
        copy.wait_send()


def on_device(n, g, tokens, cotangent, gate_weight, up_weight, down_weight_t, error_memory, q_init):
    token_rows, depth = tokens.shape
    rows, hidden = gate_weight.shape
    rank = q_init.shape[2]
    used = 3 * rank
    bits = n.bit_length() - 1
    padded = -(-rows // LANES) * LANES
    q_pad = jnp.stack(
        [jnp.pad(q_init[m], ((0, 0), (m * rank, LANES - (m + 1) * rank))) for m in range(3)]
    )
    c_blocks = min(n, hidden // LANES)
    chunk = (used // (n // c_blocks), hidden // c_blocks)
    copies = 12 * (n - 1) + 3 * (n - 1) + 2 * (g - 1)
    recv_shapes = [
        pltpu.VMEM((3, 1 << (bits - 1 - t), rows, hidden), BF16) for t in range(bits)
    ]
    vmem = pl.BlockSpec(memory_space=pltpu.VMEM)
    token_grad, new_error, hats, q_t = pl.pallas_call(
        functools.partial(kernel, n, g, rank, bits),
        out_shape=(
            jax.ShapeDtypeStruct((token_rows, depth), BF16),
            jax.ShapeDtypeStruct((1, rows, 3 * hidden), BF16),
            jax.ShapeDtypeStruct((rows, LANES), F32),
            jax.ShapeDtypeStruct((used, hidden), F32),
        ),
        in_specs=[vmem] * 7,
        out_specs=(vmem,) * 4,
        scratch_shapes=[
            pltpu.VMEM((3, depth, hidden), BF16),
            pltpu.VMEM((depth, token_rows), BF16),
            pltpu.VMEM((depth, token_rows), BF16),
            pltpu.VMEM((token_rows, hidden), F32),
            pltpu.VMEM((token_rows, hidden), F32),
            pltpu.VMEM((token_rows, hidden), BF16),
            pltpu.VMEM((token_rows, hidden), BF16),
            pltpu.VMEM((token_rows, hidden), BF16),
            pltpu.VMEM((3, depth, hidden), BF16),
            *recv_shapes,
            pltpu.VMEM((3, padded, hidden), F32),
            pltpu.VMEM((padded, LANES), F32),
            pltpu.VMEM((padded, LANES), F32),
            pltpu.VMEM((LANES, LANES), F32),
            pltpu.VMEM((LANES, hidden), F32),
            pltpu.VMEM((g, rows, LANES), BF16),
            pltpu.VMEM((n, rank, LANES), F32),
            pltpu.VMEM((n,) + chunk, BF16),
            pltpu.VMEM((n,) + chunk, BF16),
            pltpu.VMEM((g,) + chunk, BF16),
            pltpu.VMEM((n,) + chunk, BF16),
            pltpu.SemaphoreType.DMA((copies,)),
            pltpu.SemaphoreType.DMA((copies,)),
            pltpu.SemaphoreType.DMA((3,)),
        ],
        compiler_params=pltpu.CompilerParams(
            collective_id=0, has_side_effects=True, vmem_limit_bytes=67_043_328
        ),
    )(tokens, cotangent, gate_weight, up_weight, down_weight_t, error_memory, q_pad)
    p_hat = jnp.stack([hats[:, m * rank:(m + 1) * rank] for m in range(3)])
    q_new = q_t.reshape(3, rank, hidden).transpose(0, 2, 1)
    return token_grad, new_error, p_hat, q_new


def solution(mesh):
    return jax.shard_map(
        functools.partial(on_device, mesh.shape["node"], mesh.shape["grp"]),
        mesh=mesh,
        in_specs=(
            P(("node", "grp"), None),
            P(("node", "grp"), None),
            P("node", None),
            P("node", None),
            P("node", None),
            P("grp", "node", None),
            P(),
        ),
        out_specs=(P(("node", "grp"), None), P("grp", "node", None), P(None, "node", None), P()),
        check_vma=False,
    )
```

profile of v0, /device:TPU:0, one launch (start us, length us, event | category | flops | bytes accessed | tf_op | source)
XLA Modules:
  0.0 149.1 jit_solution(5493146110265331606)
XLA Ops:
  0.6 1.1 fusion
  1.7 0.2 copy.21
  1.9 0.2 copy.22
  2.1 0.2 copy.23
  2.3 0.3 pad_bitcast_fusion
  2.7 1.3 pad_maximum_fusion.q_pad
  4.0 138.4 %shard_map.102 = (bf16[384,1792]{1,0:T(8,128)(2,1)}, bf16[1,224,3072]{2,1,0:T(8,128)(2,1)}, f32[224,128]{1,0:T(8,128)}, f32[96,1024]{1,0:T(8,128)}) custom-call(bf16[384,1792]{1,0:T(8,128)(2,1)} %tok.1, bf16[384,1792]{1,0:T(8,128)(2,1)} %cot.1, bf16[224,1024]{1,0:T(8,128)(2,1)} %w_gate.1, bf16[224,1024]{1,0:T(8,128)(2,1)} %w_up.1, bf16[224,1024]{1,0:T(8,128)(2,1)} %w_down.1, ...), custom_call_target="tpu_custom_call" | custom-call | tf_op jit(solution)/shard_map/pallas_call | solution.py:370
  142.4 1.2 slice_bitcast_fusion.2
  143.6 0.1 copy.18
  143.7 0.1 copy.20
  143.7 0.1 copy.19
  143.8 0.7 pad_maximum_fusion.1
  144.5 0.0 copy-start
  144.5 2.6 %copy.27 = bf16[384,1792]{1,0:T(8,128)(2,1)} copy(bf16[384,1792]{1,0:T(8,128)(2,1)} %get-tuple-element.28) | data formatting | bytes 2752512
  147.1 0.0 copy-done
  147.1 0.0 copy-start.1
  147.1 1.1 copy.28
  148.2 0.2 copy-done.1
  148.3 0.7 copy.29
  (1 shorter events, 0.0 us)
Async XLA Ops:
  144.5 2.6 %copy-start = (bf16[1,224,3072]{2,1,0:T(8,128)(2,1)S(1)}, bf16[1,224,3072]{2,1,0:T(8,128)(2,1)}, u32[]{:S(2)}) copy-start(bf16[1,224,3072]{2,1,0:T(8,128)(2,1)} %get-tuple-element.29) | copy-start | bytes 4128772
  147.1 1.2 copy-start.1
where the time goes:
time: 149 us
  Pallas kernels  138 us (93%)
  local copies, waits for them, and re-layouts  8 us (5%)
  other arithmetic  1.93 us (1%)
    pallas_call x1, Pallas kernels, on_device(): pl.pallas_call(functools.partial(kernel, n, g, rank, bits), out_shape=(ja...  138 us
    unnamed x10, local copies, waits for them, and re-layouts  5.18 us

commit v1 on v0

v1 whole, which is shorter than its diff:
```python
import functools
import math

import jax
import jax.numpy as jnp
from jax import lax
from jax.experimental import pallas as pl
from jax.experimental.pallas import tpu as pltpu
from jax.sharding import PartitionSpec as P

MESH = pl.DeviceIdType.MESH
F32, BF16 = jnp.float32, jnp.bfloat16
HIGHEST = lax.Precision.HIGHEST
LANES = 128


def gelu_parts(value):
    coeff = math.sqrt(2.0 / math.pi)
    square = value * value
    tanh_value = jnp.tanh(coeff * (value + 0.044715 * square * value))
    activation = 0.5 * value * (1.0 + tanh_value)
    slope = 0.5 * (1.0 + tanh_value) + 0.5 * value * (1.0 - tanh_value * tanh_value) * coeff * (
        1.0 + 3.0 * 0.044715 * square
    )
    return activation, slope


def dot(a, b, precision=None):
    return jnp.dot(a, b, preferred_element_type=F32, precision=precision)


def dot_nt(a, b, precision=None):
    return lax.dot_general(
        a, b, (((1,), (1,)), ((), ())), preferred_element_type=F32, precision=precision
    )


def subsets(items):
    found = [()]
    for item in items:
        found += [s + (item,) for s in found]
    return found


def kernel(
    n, g, rank,
    tok_hbm, cot_hbm, w_gate, w_up, w_down, err_hbm, q_hbm,
    tok_grad, new_err, p_out, q_out,
    full, tok, cot, turned, turned_in, acts, ups, mine, theirs, grads, *rest
):
    bits = n.bit_length() - 1
    recv_bufs = rest[:bits - 1]
    (high, low, q_right, err, q_rows, tok_out, err_out, pw_acc, power, block_diag, q_t, pw_all,
     gram_all, q_part, q_rs, q_grp, q_all, send_sems, recv_sems, local_sems) = rest[bits - 1:]
    me, grp = lax.axis_index("node"), lax.axis_index("grp")
    rows, hidden = w_gate.shape
    tokens, depth = tok.shape
    side = depth // 2
    wide = 2 * LANES
    chunks = hidden // wide
    used = 3 * rank
    weights = (w_gate, w_up, w_down)

    barrier = pltpu.get_barrier_semaphore()
    for d in range(1, n):
        pl.semaphore_signal(barrier, inc=1, device_id=(lax.rem(me + d, n), grp), device_id_type=MESH)
    for d in range(1, g):
        pl.semaphore_signal(barrier, inc=1, device_id=(me, lax.rem(grp + d, g)), device_id_type=MESH)

    flip = [(1 << b) * (1 - 2 * lax.rem(me // (1 << b), 2)) for b in range(bits)]
    offset = lambda mask: sum((flip[b] for b in mask), 0)
    pair = me + flip[0]
    core = lax.rem(me, 2)
    half_node = me // 2
    half_flip = [0] + [
        (1 << (b - 1)) * (1 - 2 * lax.rem(me // (1 << b), 2)) for b in range(1, bits)
    ]
    half_offset = lambda mask: sum((half_flip[b] for b in mask), 0)
    plane = lax.rem(grp, 2)
    twin = grp + 1 - 2 * plane
    outer = list(range(1, bits))
    orders = [outer, outer[::-1]]
    steps = len(outer)
    block = lambda index: pl.ds(pl.multiple_of(index * rows, rows), rows)

    locals_count = [0]

    def local(src, dst):
        copy = pltpu.make_async_copy(src, dst, local_sems.at[locals_count[0]])
        locals_count[0] += 1
        copy.start()
        return copy

    loads = []
    for c in range(chunks):
        loads.append([
            local(weights[w].at[:, pl.ds(j * LANES, LANES)], full.at[j, w, block(me)])
            for j in (2 * c, 2 * c + 1) for w in range(3)
        ])
    cot_load = local(cot_hbm, cot)
    tok_load = local(tok_hbm, tok)
    q_load = local(q_hbm, q_rows.at[0:used])
    err_load = local(err_hbm.at[0], err)

    count = [0]
    started = []

    def send(src, dst, node, group):
        copy = pltpu.make_async_remote_copy(
            src_ref=src, dst_ref=dst,
            send_sem=send_sems.at[count[0]], recv_sem=recv_sems.at[count[0]],
            device_id=(node, group), device_id_type=MESH,
        )
        count[0] += 1
        started.append(copy)
        copy.start()
        return copy

    if rows % 32 == 0:
        parts = [[(0, rows // 2, 0), (rows // 2, rows // 2, 1)]] * chunks
    else:
        parts = [[(0, rows, c % 2)] for c in range(chunks)]

    def piece(j, mask, part):
        start = (me + offset(mask)) * rows + part[0]
        return full.at[j, :, pl.ds(pl.multiple_of(start, math.gcd(rows, part[1])), part[1]), :]

    arrivals, across, inside = {}, {}, {}

    def gather_send(c, t, part):
        order = orders[part[2]]
        for mask in subsets(order[:t]):
            at = piece(2 * c + plane, mask, part)
            copy = send(at, at, me + flip[order[t]], grp)
            arrivals.setdefault((c, t, part), []).append((copy, mask + (order[t],)))

    def gather_step(c, t):
        for part in parts[c]:
            for copy, _ in arrivals[c, t, part]:
                copy.wait_recv()
            if t + 1 < steps:
                gather_send(c, t + 1, part)
            for _, mask in arrivals[c, t, part]:
                at = piece(2 * c + plane, mask, part)
                across.setdefault(c, []).append((send(at, at, me, twin), mask, part))
                inside.setdefault(c, []).append(send(at, at, pair, grp))

    def gather_finish(c):
        for copy, mask, part in across[c]:
            copy.wait_recv()
            at = piece(2 * c + 1 - plane, mask, part)
            inside[c].append(send(at, at, pair, grp))
        for copy in inside[c]:
            copy.wait_recv()

    pl.semaphore_wait(barrier, n - 1 + g - 1)

    def launch(c):
        for copy in loads[c]:
            copy.wait()
        for part in parts[c]:
            gather_send(c, 0, part)
        at = full.at[pl.ds(2 * c, 2), :, block(me), :]
        inside.setdefault(c, []).append(send(at, at, pair, grp))

    for c in range(min(2, chunks)):
        launch(c)

    pw_acc[...] = jnp.zeros_like(pw_acc)
    power[...] = jnp.zeros_like(power)
    block_diag[...] = jnp.zeros_like(block_diag)
    q_t[...] = jnp.zeros_like(q_t)
    for buf in (high, low):
        for m in range(3):
            buf[m, rows:, :] = jnp.zeros((buf.shape[1] - rows, hidden), BF16)

    def turn(which, i):
        src = (tok, cot)[which]
        tile = src[:, i * wide:(i + 1) * wide].T
        first = i * wide
        while first < (i + 1) * wide:
            b = first // rows
            last = min((b + 1) * rows, (i + 1) * wide)
            at = (b // 2) * rows + first - b * rows
            turned[which, b % 2, at:at + last - first, :] = tile[first - i * wide:last - i * wide]
            first = last

    def right_factors():
        q_load.wait()
        q_rows[used:, :] = jnp.zeros((LANES - used, hidden), F32)
        lane = lax.broadcasted_iota(jnp.int32, (wide, LANES), 1)
        for c in range(chunks):
            at = slice(c * wide, (c + 1) * wide)
            columns = q_rows[:, at].T
            top = columns.astype(BF16)
            bottom = (columns - top.astype(F32)).astype(BF16)
            for m in range(3):
                inside_m = (lane >= m * rank) & (lane < (m + 1) * rank)
                q_right[m, at, 0:LANES] = jnp.where(inside_m, top.astype(F32), 0.0).astype(BF16)
                q_right[m, at, LANES:] = jnp.where(inside_m, bottom.astype(F32), 0.0).astype(BF16)

    filler = []
    for which, load in ((1, cot_load), (0, tok_load)):
        filler.append(load.wait)
        for i in range(depth // wide):
            filler.append(functools.partial(turn, which, i))
        filler.append(lambda which=which: turned_sends.append(
            send(turned.at[which, 1 - core], turned_in.at[which], pair, grp)))
    filler.append(right_factors)
    turned_sends = []

    events = sorted(
        ((c, t) for c in range(chunks) for t in range(steps)), key=lambda e: (2 * e[1] + e[0], -e[1])
    )
    each = -(-len(filler) // len(events))
    for c, t in events:
        for work in filler[:each]:
            work()
        filler = filler[each:]
        gather_step(c, t)
        if t == 0 and c + 2 < chunks:
            launch(c + 2)
    for work in filler:
        work()

    def columns_of(c, w):
        return jnp.concatenate([full[2 * c, w], full[2 * c + 1, w]], axis=1)

    def forward(c):
        acts[...] = dot(tok[...], columns_of(c, 0))
        up_pre = dot(tok[...], columns_of(c, 1))
        activation, slope = gelu_parts(acts[...])
        acts[...] = activation
        ups[...] = up_pre * slope
        mine[c, 0] = (activation * up_pre).astype(BF16)

    def backward(c):
        back = dot(cot[...], columns_of(c, 2))
        mine[c, 1] = (back * ups[...]).astype(BF16)
        mine[c, 2] = (back * acts[...]).astype(BF16)

    tile = side // 2

    def gradient(c, m):
        which, k = (1, 0) if m == 2 else (0, m + 1)
        right = jnp.concatenate([mine[c, k], theirs[c, k]], axis=0)
        for i in range(2):
            at = pl.ds(i * tile, tile)
            left = jnp.concatenate([turned[which, core, at, :], turned_in[which, at, :]], axis=1)
            part = dot(left, right).astype(BF16)
            grads[c, m, 0, at, :] = part[:, 0:LANES]
            grads[c, m, 1, at, :] = part[:, LANES:]

    reduces = {}

    def reduce_start(c, m, t):
        for h in range(2):
            bit = orders[h][t]
            reduces[c, m, t, h] = []
            for slot, mask in enumerate(subsets(orders[h][t + 1:])):
                src = grads.at[c, m, h, block(half_node + half_flip[bit] + half_offset(mask))]
                dst = recv_bufs[t].at[(c * 3 + m) * 2 + h, slot]
                reduces[c, m, t, h].append(send(src, dst, me + flip[bit], grp))

    scale = 1.0 / math.sqrt(tokens * n)

    def reduce_add(c, m, t):
        for h in range(2):
            for slot, mask in enumerate(subsets(orders[h][t + 1:])):
                reduces[c, m, t, h][slot].wait_recv()
                at = block(half_node + half_offset(mask))
                total = (
                    grads[c, m, h, at, :].astype(F32)
                    + recv_bufs[t][(c * 3 + m) * 2 + h, slot].astype(F32)
                )
                if t < steps - 1:
                    grads[c, m, h, at, :] = total.astype(BF16)
                else:
                    first = c * wide + h * LANES
                    memory = err[:, m * hidden + first:m * hidden + first + LANES].astype(F32)
                    merged = total * scale + memory
                    top = merged.astype(BF16)
                    high[m, 0:rows, first:first + LANES] = top
                    low[m, 0:rows, first:first + LANES] = (merged - top.astype(F32)).astype(BF16)

    def advance(c, m, t):
        reduce_add(c, m, t - 1)
        reduce_start(c, m, t)

    def reduce_finish(c, m):
        reduce_add(c, m, steps - 1)
        at = slice(c * wide, (c + 1) * wide)
        both = dot(high[m, 0:rows, at], q_right[m, at, :])
        rest_part = dot(low[m, 0:rows, at], q_right[m, at, 0:LANES])
        pw_acc[...] += both[:, 0:LANES] + both[:, LANES:] + rest_part

    def token_part(i):
        at = slice(i * wide, (i + 1) * wide)
        total = jnp.zeros((tokens, wide), F32)
        for k in (1, 2):
            left = jnp.concatenate([mine[c, k] for c in range(chunks)], axis=1)
            right = jnp.concatenate([full[j, k - 1, at, :] for j in range(2 * chunks)], axis=1)
            total += dot_nt(left, right)
        tok_out[:, at] = total.astype(BF16)
        token_writes.append(local(tok_out.at[:, at], tok_grad.at[:, at]))

    token_writes = []
    token_tiles = list(range(depth // wide))

    def token_work(amount):
        for _ in range(min(amount, len(token_tiles))):
            token_part(token_tiles.pop(0))

    order_m = (2, 0, 1)
    for c in range(chunks):
        gather_finish(c)
        forward(c)
        hid_copy = send(mine.at[c, 0], theirs.at[c, 0], pair, grp)
        backward(c)
        back_copy = send(mine.at[c, pl.ds(1, 2)], theirs.at[c, pl.ds(1, 2)], pair, grp)
        if c == 0:
            err_load.wait()
            for copy in turned_sends:
                copy.wait_recv()
        hid_copy.wait_recv()
        gradient(c, 2)
        reduce_start(c, 2, 0)
        back_copy.wait_recv()
        for m in (0, 1):
            gradient(c, m)
            reduce_start(c, m, 0)
        if c > 0:
            for m in order_m:
                reduce_finish(c - 1, m)
        if c == chunks - 1:
            token_work(3)
        for t in range(1, steps):
            for m in order_m:
                advance(c, m, t)
                if c == chunks - 1:
                    token_work(2)
    token_work(len(token_tiles))
    for m in order_m:
        reduce_finish(chunks - 1, m)

    pw_all[grp] = pw_acc[...].astype(BF16)
    copies = [
        send(pw_all.at[grp], pw_all.at[grp], me, lax.rem(grp + d, g)) for d in range(1, g)
    ]
    for copy in copies:
        copy.wait_recv()
    total = pw_all[0].astype(F32)
    for k in range(1, g):
        total += pw_all[k].astype(F32)
    power[0:rows, :] = total * (1.0 / g)

    lane = lax.broadcasted_iota(jnp.int32, (rank, LANES), 1)
    row = lax.broadcasted_iota(jnp.int32, (rank, LANES), 0)
    padded = power[...]
    gram = dot(padded.T, padded, HIGHEST)
    picked = gram[0:rank]
    for m in range(1, 3):
        picked = jnp.where(lane >= m * rank, gram[m * rank:(m + 1) * rank], picked)
    gram_all[me] = picked
    copies = [
        send(gram_all.at[me], gram_all.at[me], lax.rem(me + d, n), grp) for d in range(1, n)
    ]
    for copy in copies:
        copy.wait_recv()
    picked = gram_all[0]
    for k in range(1, n):
        picked += gram_all[k]

    work = []
    for m in range(3):
        rolled = picked if m == 0 else pltpu.roll(picked, LANES - m * rank, 1)
        unit = jnp.where(lane == row + rank, 1.0, 0.0).astype(F32)
        work.append(jnp.where(lane < rank, rolled, unit))
    for j in range(rank):
        for m in range(3):
            a = work[m]
            inverse = 1.0 / jnp.sqrt(a[j:j + 1, j:j + 1])
            pivot_row = a[j:j + 1, :] * inverse
            column = a[:, j:j + 1] * inverse
            work[m] = jnp.where(row > j, a - column * pivot_row, jnp.where(row == j, pivot_row, a))
    for m in range(3):
        shift = ((m - 1) * rank) % LANES
        moved = work[m] if shift == 0 else pltpu.roll(work[m], shift, 1)
        inside_m = (lane >= m * rank) & (lane < (m + 1) * rank)
        block_diag[m * rank:(m + 1) * rank, :] = jnp.where(inside_m, moved, 0.0)
    hat_t = dot_nt(block_diag[...], power[...], HIGHEST)
    hat = dot_nt(power[0:rows, :], block_diag[...], HIGHEST)
    p_out[...] = hat_t[0:used, 0:rows]

    c_blocks = min(n, hidden // LANES)
    r_blocks = n // c_blocks
    c_size, r_size = hidden // c_blocks, used // r_blocks
    hat_top = hat_t.astype(BF16)
    hat_bottom = (hat_t - hat_top.astype(F32)).astype(BF16)
    for m in range(3):
        at = slice(m * rank, (m + 1) * rank)
        left = jnp.concatenate([hat_top[at], hat_bottom[at]], axis=0)
        both = dot(left, high[m])
        q_t[at, :] = both[0:rank] + both[rank:]
    spots = [
        (slice(c // c_blocks * r_size, (c // c_blocks + 1) * r_size),
         slice(c % c_blocks * c_size, (c % c_blocks + 1) * c_size))
        for c in range(n)
    ]
    for c in range(n):
        q_part[c] = q_t[spots[c]].astype(BF16)
    q_rs[me] = q_part[me]
    copies = []
    for d in range(1, n):
        to = lax.rem(me + d, n)
        copies.append(send(q_part.at[to], q_rs.at[me], to, grp))
    for copy in copies:
        copy.wait_recv()
    total = q_rs[0].astype(F32)
    for k in range(1, n):
        total += q_rs[k].astype(F32)
    q_grp[grp] = total.astype(BF16)
    copies = [send(q_grp.at[grp], q_grp.at[grp], me, lax.rem(grp + d, g)) for d in range(1, g)]
    for copy in copies:
        copy.wait_recv()
    total = q_grp[0].astype(F32)
    for k in range(1, g):
        total += q_grp[k].astype(F32)
    q_all[me] = (total * (1.0 / g)).astype(BF16)
    copies = [send(q_all.at[me], q_all.at[me], lax.rem(me + d, n), grp) for d in range(1, n)]
    for copy in copies:
        copy.wait_recv()
    for c in range(n):
        q_t[spots[c]] = q_all[c].astype(F32)
    q_out[...] = q_t[0:used, :]

    lanes = lax.broadcasted_iota(jnp.int32, (rows, LANES), 1)
    right = q_t[...].astype(BF16)
    right = jnp.concatenate([right, right], axis=0)
    writes = []
    for m in range(3):
        own = jnp.where((lanes >= m * rank) & (lanes < (m + 1) * rank), hat, 0.0)
        top = own.astype(BF16)
        left = jnp.concatenate([top, (own - top.astype(F32)).astype(BF16)], axis=1)
        for c in range(chunks):
            at = slice(c * wide, (c + 1) * wide)
            rebuilt = dot(left, right[:, at])
            merged = high[m, 0:rows, at].astype(F32) + low[m, 0:rows, at].astype(F32)
            err_out[:, m * hidden + c * wide:m * hidden + (c + 1) * wide] = (
                merged - rebuilt
            ).astype(BF16)
        at = pl.ds(m * hidden, hidden)
        writes.append(local(err_out.at[:, at], new_err.at[0, :, at]))
    for copy in started:
        copy.wait_send()
    for copy in token_writes + writes:
        copy.wait()


def on_device(n, g, tokens, cotangent, gate_weight, up_weight, down_weight_t, error_memory, q_init):
    token_rows, depth = tokens.shape
    rows, hidden = gate_weight.shape
    rank = q_init.shape[2]
    used = 3 * rank
    bits = n.bit_length() - 1
    side = depth // 2
    wide = 2 * LANES
    chunks = hidden // wide
    padded = -(-rows // LANES) * LANES
    q_rows = q_init.transpose(0, 2, 1).reshape(used, hidden)
    c_blocks = min(n, hidden // LANES)
    chunk = (used // (n // c_blocks), hidden // c_blocks)
    others = n // 2 - 1
    parts = 2 if rows % 32 == 0 else 1
    copies = (
        chunks * (1 + parts * 4 * others) + chunks * 6 * others + 2 * chunks + 2
        + 3 * (n - 1) + 2 * (g - 1)
    )
    copies_here = 6 * chunks + 4 + depth // wide + 3
    recv_shapes = [
        pltpu.VMEM((chunks * 6, 1 << (bits - 2 - t), rows, LANES), BF16) for t in range(bits - 1)
    ]
    vmem = pl.BlockSpec(memory_space=pltpu.VMEM)
    hbm = pl.BlockSpec(memory_space=pl.ANY)
    token_grad, new_error, hat_t, q_t = pl.pallas_call(
        functools.partial(kernel, n, g, rank),
        out_shape=(
            jax.ShapeDtypeStruct((token_rows, depth), BF16),
            jax.ShapeDtypeStruct((1, rows, 3 * hidden), BF16),
            jax.ShapeDtypeStruct((used, rows), F32),
            jax.ShapeDtypeStruct((used, hidden), F32),
        ),
        in_specs=[hbm] * 7,
        out_specs=(hbm, hbm, vmem, vmem),
        scratch_shapes=[
            pltpu.VMEM((2 * chunks, 3, depth, LANES), BF16),
            pltpu.VMEM((token_rows, depth), BF16),
            pltpu.VMEM((token_rows, depth), BF16),
            pltpu.VMEM((2, 2, side, token_rows), BF16),
            pltpu.VMEM((2, side, token_rows), BF16),
            pltpu.VMEM((token_rows, wide), F32),
            pltpu.VMEM((token_rows, wide), F32),
            pltpu.VMEM((chunks, 3, token_rows, wide), BF16),
            pltpu.VMEM((chunks, 3, token_rows, wide), BF16),
            pltpu.VMEM((chunks, 3, 2, side, LANES), BF16),
            *recv_shapes,
            pltpu.VMEM((3, padded, hidden), BF16),
            pltpu.VMEM((3, padded, hidden), BF16),
            pltpu.VMEM((3, hidden, wide), BF16),
            pltpu.VMEM((rows, 3 * hidden), BF16),
            pltpu.VMEM((LANES, hidden), F32),
            pltpu.VMEM((token_rows, depth), BF16),
            pltpu.VMEM((rows, 3 * hidden), BF16),
            pltpu.VMEM((rows, LANES), F32),
            pltpu.VMEM((padded, LANES), F32),
            pltpu.VMEM((LANES, LANES), F32),
            pltpu.VMEM((LANES, hidden), F32),
            pltpu.VMEM((g, rows, LANES), BF16),
            pltpu.VMEM((n, rank, LANES), F32),
            pltpu.VMEM((n,) + chunk, BF16),
            pltpu.VMEM((n,) + chunk, BF16),
            pltpu.VMEM((g,) + chunk, BF16),
            pltpu.VMEM((n,) + chunk, BF16),
            pltpu.SemaphoreType.DMA((copies,)),
            pltpu.SemaphoreType.DMA((copies,)),
            pltpu.SemaphoreType.DMA((copies_here,)),
        ],
        compiler_params=pltpu.CompilerParams(
            collective_id=0, has_side_effects=True, vmem_limit_bytes=67_043_328
        ),
    )(tokens, cotangent, gate_weight, up_weight, down_weight_t, error_memory, q_rows)
    p_hat = hat_t.reshape(3, rank, rows).transpose(0, 2, 1)
    q_new = q_t.reshape(3, rank, hidden).transpose(0, 2, 1)
    return token_grad, new_error, p_hat, q_new


def solution(mesh):
    return jax.shard_map(
        functools.partial(on_device, mesh.shape["node"], mesh.shape["grp"]),
        mesh=mesh,
        in_specs=(
            P(("node", "grp"), None),
            P(("node", "grp"), None),
            P("node", None),
            P("node", None),
            P("node", None),
            P("grp", "node", None),
            P(),
        ),
        out_specs=(P(("node", "grp"), None), P("grp", "node", None), P(None, "node", None), P()),
        check_vma=False,
    )
```

time: 149 us -> 130 us (0.87)
  Pallas kernels: 138 us -> 124 us
  local copies, waits for them, and re-layouts: 8 us -> 5.09 us
  other arithmetic: 1.93 us -> 0 us
    pallas_call x1, Pallas kernels: 138 us -> 124 us  [on_device(): pl.pallas_call(functools.partial(kernel, n, g, rank), out_shape=(jax.Shap...]
    another operation x2 -> x0, other arithmetic: 1.93 us -> none  [the longest x1 1.26 us: on_device(): jnp.stack([jnp.pad(q_init[m], ((0, 0), (m * rank, LANES - (m + 1) * rank)...]
    another operation x6 -> x0, local copies, waits for them, and re-layouts: 1.77 us -> none  [the longest x4 1.38 us: on_device(): p_hat = jnp.stack([hats[:, m * rank:(m + 1) * rank] for m in range(3)])]
where the time goes in v1:
time: 130 us
  Pallas kernels  124 us (95%)
  local copies, waits for them, and re-layouts  5.09 us (4%)
    pallas_call x1, Pallas kernels, on_device(): pl.pallas_call(functools.partial(kernel, n, g, rank), out_shape=(jax.Shap...  124 us
    unnamed x10, local copies, waits for them, and re-layouts  5.09 us

profile of v1, /device:TPU:0, one launch (start us, length us, event | category | flops | bytes accessed | tf_op | source)
XLA Modules:
  0.0 129.6 jit_solution(15134640082705774357)
XLA Ops:
  0.6 123.9 %shard_map.102 = (bf16[384,1792]{1,0:T(8,128)(2,1)}, bf16[1,224,3072]{2,1,0:T(8,128)(2,1)}, f32[96,224]{1,0:T(8,128)}, f32[96,1024]{1,0:T(8,128)}) custom-call(bf16[384,1792]{1,0:T(8,128)(2,1)} %tok_hbm.1, bf16[384,1792]{1,0:T(8,128)(2,1)} %cot_hbm.1, bf16[224,1024]{1,0:T(8,128)(2,1)} %w_gate.1, bf16[224,1024]{1,0:T(8,128)(2,1)} %w_up.1, ...), custom_call_target="tpu_custom_call" | custom-call | tf_op jit(solution)/shard_map/pallas_call | solution.py:485
  124.5 0.0 copy-start
  124.6 2.6 %copy.15 = bf16[384,1792]{1,0:T(8,128)(2,1)} copy(bf16[384,1792]{1,0:T(8,128)(2,1)} %get-tuple-element.16) | data formatting | bytes 2752512
  127.2 0.0 copy-done
  127.2 0.0 copy-start.2
  127.2 0.0 copy-start.1
  127.2 1.1 copy.16
  128.3 0.0 copy-done.2
  128.3 0.6 copy.17
  128.9 0.0 copy-done.1
  128.9 0.7 copy.18
Async XLA Ops:
  124.5 2.6 %copy-start = (bf16[1,224,3072]{2,1,0:T(8,128)(2,1)S(1)}, bf16[1,224,3072]{2,1,0:T(8,128)(2,1)}, u32[]{:S(2)}) copy-start(bf16[1,224,3072]{2,1,0:T(8,128)(2,1)} %get-tuple-element.17) | copy-start | bytes 4128772
  127.2 1.1 copy-start.2
  127.2 1.7 %copy-start.1 = (f32[96,1024]{1,0:T(8,128)S(1)}, f32[96,1024]{1,0:T(8,128)}, u32[]{:S(2)}) copy-start(f32[96,1024]{1,0:T(8,128)} %get-tuple-element.11) | copy-start | bytes 1179652

commit v2 on v1

v2 whole, which is shorter than its diff:
```python
import functools
import math

import jax
import jax.numpy as jnp
from jax import lax
from jax.experimental import pallas as pl
from jax.experimental.pallas import tpu as pltpu
from jax.sharding import PartitionSpec as P

MESH = pl.DeviceIdType.MESH
F32, BF16 = jnp.float32, jnp.bfloat16
HIGHEST = lax.Precision.HIGHEST
AHEAD, LAG = 2, 2
LANES = 128


def gelu_parts(value):
    coeff = math.sqrt(2.0 / math.pi)
    square = value * value
    tanh_value = jnp.tanh(coeff * (value + 0.044715 * square * value))
    activation = 0.5 * value * (1.0 + tanh_value)
    slope = 0.5 * (1.0 + tanh_value) + 0.5 * value * (1.0 - tanh_value * tanh_value) * coeff * (
        1.0 + 3.0 * 0.044715 * square
    )
    return activation, slope


def dot(a, b, precision=None):
    return jnp.dot(a, b, preferred_element_type=F32, precision=precision)


def dot_nt(a, b, precision=None):
    return lax.dot_general(
        a, b, (((1,), (1,)), ((), ())), preferred_element_type=F32, precision=precision
    )


def subsets(items):
    found = [()]
    for item in items:
        found += [s + (item,) for s in found]
    return found


def kernel(
    n, g, rank,
    tok_hbm, cot_hbm, w_gate, w_up, w_down, err_hbm, q_hbm,
    tok_grad, new_err, p_out, q_out,
    full, tok, cot, turned, turned_in, acts, mine_hid, their_hid, mine_back,
    their_back, grads, *rest
):
    bits = n.bit_length() - 1
    recv_bufs = rest[:bits - 1]
    (high, low, q_right, err, q_rows, tok_out, err_out, pw_acc, power, block_diag, q_t, pw_all,
     gram_all, q_part, q_rs, q_grp, q_all, send_sems, recv_sems, local_sems) = rest[bits - 1:]
    me, grp = lax.axis_index("node"), lax.axis_index("grp")
    rows, hidden = w_gate.shape
    tokens, depth = tok.shape
    side = depth // 2
    wide = 2 * LANES
    chunks = hidden // wide
    blocks = hidden // LANES
    used = 3 * rank
    weights = (w_gate, w_up, w_down)

    barrier = pltpu.get_barrier_semaphore()
    for d in range(1, n):
        pl.semaphore_signal(barrier, inc=1, device_id=(lax.rem(me + d, n), grp), device_id_type=MESH)
    for d in range(1, g):
        pl.semaphore_signal(barrier, inc=1, device_id=(me, lax.rem(grp + d, g)), device_id_type=MESH)

    flip = [(1 << b) * (1 - 2 * lax.rem(me // (1 << b), 2)) for b in range(bits)]
    offset = lambda mask: sum((flip[b] for b in mask), 0)
    pair = me + flip[0]
    core = lax.rem(me, 2)
    half_node = me // 2
    half_flip = [0] + [
        (1 << (b - 1)) * (1 - 2 * lax.rem(me // (1 << b), 2)) for b in range(1, bits)
    ]
    half_offset = lambda mask: sum((half_flip[b] for b in mask), 0)
    plane = lax.rem(grp, 2)
    twin = grp + 1 - 2 * plane
    outer = list(range(1, bits))
    orders = [outer, outer[::-1]]
    steps = len(outer)
    block = lambda index: pl.ds(pl.multiple_of(index * rows, rows), rows)

    def local(src, dst, index):
        copy = pltpu.make_async_copy(src, dst, local_sems.at[index])
        copy.start()
        return copy

    for c in range(chunks):
        for j in (2 * c, 2 * c + 1):
            for w in range(3):
                local(weights[w].at[:, pl.ds(j * LANES, LANES)], full.at[j, w, block(me)], c)
    cot_load = local(cot_hbm, cot, chunks)
    tok_load = local(tok_hbm, tok, chunks + 1)
    q_load = local(q_hbm, q_rows.at[0:used], chunks + 2)
    err_load = local(err_hbm.at[0], err, chunks + 3)

    arrive_index, leave_index, leave_refs = {}, {}, {}

    def send(src, dst, node, group, arrive, leave):
        pltpu.make_async_remote_copy(
            src_ref=src, dst_ref=dst,
            send_sem=send_sems.at[leave_index.setdefault(leave, len(leave_index))],
            recv_sem=recv_sems.at[arrive_index.setdefault(arrive, len(arrive_index))],
            device_id=(node, group), device_id_type=MESH,
        ).start()

    def whole(ref, arrive, leave):
        return pltpu.make_async_remote_copy(
            src_ref=ref, dst_ref=ref,
            send_sem=send_sems.at[leave_index[leave]], recv_sem=recv_sems.at[arrive_index[arrive]],
            device_id=(me, twin), device_id_type=MESH,
        )

    def wait_all(ref, arrive, leave):
        leave_refs.setdefault(leave, (ref, arrive))
        whole(ref, arrive, leave).wait_recv()

    if rows % 32 == 0:
        parts = [[(0, rows // 2, 0), (rows // 2, rows // 2, 1)]] * chunks
    else:
        parts = [[(0, rows, c % 2)] for c in range(chunks)]

    def piece(j, mask, part):
        start = (me + offset(mask)) * rows + part[0]
        return full.at[j, :, pl.ds(pl.multiple_of(start, math.gcd(rows, part[1])), part[1]), :]

    def column_block(side_of, c):
        return 2 * c + (plane if side_of == 0 else 1 - plane)

    def new_masks(t, order):
        return [mask + (order[t],) for mask in subsets(order[:t])]

    def gather_send(c, t, part):
        order = orders[part[2]]
        for mask in subsets(order[:t]):
            at = piece(2 * c + plane, mask, part)
            send(at, at, me + flip[order[t]], grp, ("plane", c, t, part), "plane")

    def gather_step(c, t):
        for part in parts[c]:
            wait_all(full.at[2 * c, :, 0:part[1] << t, :], ("plane", c, t, part), "plane")
            if t + 1 < steps:
                gather_send(c, t + 1, part)
            for mask in new_masks(t, orders[part[2]]):
                at = piece(2 * c + plane, mask, part)
                send(at, at, me, twin, ("twin", c, t), "twin")
                send(at, at, pair, grp, ("pair", 0, c), "pair")

    def relay(c):
        for t in range(steps):
            wait_all(full.at[2 * c, :, 0:rows << t, :], ("twin", c, t), "twin")
            for part in parts[c]:
                for mask in new_masks(t, orders[part[2]]):
                    at = piece(2 * c + 1 - plane, mask, part)
                    send(at, at, pair, grp, ("pair", 1, c), "pair")

    pl.semaphore_wait(barrier, n - 1 + g - 1)

    def launch(c):
        at = full.at[pl.ds(2 * c, 2), :, block(me), :]
        pltpu.make_async_copy(at, at, local_sems.at[c]).wait()
        for part in parts[c]:
            gather_send(c, 0, part)
        for side_of in range(2):
            at = full.at[column_block(side_of, c), :, block(me), :]
            send(at, at, pair, grp, ("pair", side_of, c), "pair")

    for c in range(min(2, chunks)):
        launch(c)

    pw_acc[...] = jnp.zeros_like(pw_acc)
    power[...] = jnp.zeros_like(power)
    block_diag[...] = jnp.zeros_like(block_diag)
    q_t[...] = jnp.zeros_like(q_t)
    for buf in (high, low):
        for m in range(3):
            for j in range(blocks):
                buf[m, j, rows:, :] = jnp.zeros((buf.shape[2] - rows, LANES), BF16)

    def turn(which, i):
        src = (tok, cot)[which]
        tile = src[:, i * wide:(i + 1) * wide].T
        first = i * wide
        while first < (i + 1) * wide:
            b = first // rows
            last = min((b + 1) * rows, (i + 1) * wide)
            at = (b // 2) * rows + first - b * rows
            turned[which, b % 2, at:at + last - first, :] = tile[first - i * wide:last - i * wide]
            first = last

    def right_factors():
        q_load.wait()
        q_rows[used:, :] = jnp.zeros((LANES - used, hidden), F32)
        lane = lax.broadcasted_iota(jnp.int32, (wide, LANES), 1)
        for c in range(chunks):
            at = slice(c * wide, (c + 1) * wide)
            columns = q_rows[:, at].T
            top = columns.astype(BF16)
            bottom = (columns - top.astype(F32)).astype(BF16)
            for m in range(3):
                inside_m = (lane >= m * rank) & (lane < (m + 1) * rank)
                q_right[m, at, 0:LANES] = jnp.where(inside_m, top.astype(F32), 0.0).astype(BF16)
                q_right[m, at, LANES:] = jnp.where(inside_m, bottom.astype(F32), 0.0).astype(BF16)

    filler = []
    for which, load in ((1, cot_load), (0, tok_load)):
        filler.append(load.wait)
        for i in range(depth // wide):
            filler.append(functools.partial(turn, which, i))
        filler.append(functools.partial(
            send, turned.at[which, 1 - core], turned_in.at[which], pair, grp, "turned", "turned"))
    filler.append(right_factors)

    def forward(j):
        both = dot(tok[...], jnp.concatenate([full[j, 0], full[j, 1]], axis=1))
        acts[...] = both
        up_pre = acts[:, LANES:]
        activation, slope = gelu_parts(acts[:, 0:LANES])
        mine_hid[j] = (activation * up_pre).astype(BF16)
        acts[:, LANES:] = activation
        acts[:, 0:LANES] = up_pre * slope

    def backward(j):
        back = dot(cot[...], full[j, 2])
        mine_back[j, :, 0:LANES] = (back * acts[:, 0:LANES]).astype(BF16)
        mine_back[j, :, LANES:] = (back * acts[:, LANES:]).astype(BF16)

    tile = side // 2
    group_m = ((2,), (0, 1))

    def gradient(u, j, k):
        own, other = ((mine_hid, their_hid), (mine_back, their_back))[k]
        right = jnp.concatenate([own[j], other[j]], axis=0)
        for i in range(2):
            at = pl.ds(i * tile, tile)
            left = jnp.concatenate([turned[1 - k, core, at, :], turned_in[1 - k, at, :]], axis=1)
            part = dot(left, right).astype(BF16)
            for i, m in enumerate(group_m[k]):
                grads[u, m, at, :] = part[:, i * LANES:(i + 1) * LANES]

    slots_of = {2: 0, 0: 1, 1: 2}

    def reduce_start(u, k, t):
        for m in group_m[k]:
            for first, size, h in parts[u % chunks]:
                bit = orders[h][t]
                for slot, mask in enumerate(subsets(orders[h][t + 1:])):
                    at = half_node + half_flip[bit] + half_offset(mask)
                    at = pl.ds(pl.multiple_of(at * rows + first, math.gcd(rows, size)), size)
                    dst = recv_bufs[t].at[u * 3 + slots_of[m], slot, pl.ds(first, size)]
                    send(grads.at[u, m, at], dst, me + flip[bit], grp,
                         ("reduce", u, k, t), ("reduce", t))

    scale = 1.0 / math.sqrt(tokens * n)

    def reduce_add(u, j, k, t):
        wait_all(
            recv_bufs[t].at[pl.ds(u * 3 + k, 1 + k)], ("reduce", u, k, t), ("reduce", t))
        for m in group_m[k]:
            for first, size, h in parts[u % chunks]:
                for slot, mask in enumerate(subsets(orders[h][t + 1:])):
                    at = (half_node + half_offset(mask)) * rows + first
                    at = pl.ds(pl.multiple_of(at, math.gcd(rows, size)), size)
                    total = (
                        grads[u, m, at, :].astype(F32)
                        + recv_bufs[t][u * 3 + slots_of[m], slot, first:first + size].astype(F32)
                    )
                    if t < steps - 1:
                        grads[u, m, at, :] = total.astype(BF16)
                    else:
                        span = pl.ds(pl.multiple_of(m * hidden + j * LANES, LANES), LANES)
                        memory = err[first:first + size, span].astype(F32)
                        merged = total * scale + memory
                        top = merged.astype(BF16)
                        high[m, j, first:first + size] = top
                        low[m, j, first:first + size] = (merged - top.astype(F32)).astype(BF16)

    def reduce_finish(u, j, k):
        reduce_add(u, j, k, steps - 1)
        at = pl.ds(pl.multiple_of(j * LANES, LANES), LANES)
        for m in group_m[k]:
            both = dot(high[m, j, 0:rows], q_right[m, at, :])
            rest_part = dot(low[m, j, 0:rows], q_right[m, at, 0:LANES])
            pw_acc[...] += both[:, 0:LANES] + both[:, LANES:] + rest_part

    def token_part(i):
        at = slice(i * wide, (i + 1) * wide)
        total = jnp.zeros((tokens, wide), F32)
        for k in range(2):
            lanes_k = slice(k * LANES, (k + 1) * LANES)
            left = jnp.concatenate([mine_back[j, :, lanes_k] for j in range(blocks)], axis=1)
            right = jnp.concatenate([full[j, k, at, :] for j in range(blocks)], axis=1)
            total += dot_nt(left, right)
        tok_out[:, at] = total.astype(BF16)
        local(tok_out.at[:, at], tok_grad.at[:, at], chunks + 4)

    token_tiles = list(range(depth // wide))

    def token_work(amount):
        for _ in range(min(amount, len(token_tiles))):
            token_part(token_tiles.pop(0))

    units = [(0, c) for c in range(chunks)]
    for c in range(chunks):
        units.insert(min(chunks - 1 + 2 * c, len(units)), (1, c))

    def prepare(u):
        side_of, c = units[u]
        wait_all(full.at[2 * c, :, 0:side, :], ("pair", side_of, c), "pair")
        j = column_block(*units[u])
        forward(j)
        send(mine_hid.at[j], their_hid.at[j], pair, grp, ("hidden", u), "hidden")
        backward(j)
        send(mine_back.at[j], their_back.at[j], pair, grp, ("back", u), "back")

    def reduce_all(u):
        j = column_block(*units[u])
        wait_all(their_hid.at[j], ("hidden", u), "hidden")
        gradient(u, j, 0)
        reduce_start(u, 0, 0)
        wait_all(their_back.at[j], ("back", u), "back")
        gradient(u, j, 1)
        reduce_start(u, 1, 0)

    def advance(u, t):
        j = column_block(*units[u])
        for k in range(2):
            reduce_add(u, j, k, t - 1)
            reduce_start(u, k, t)

    def finish(u):
        j = column_block(*units[u])
        for k in range(2):
            reduce_finish(u, j, k)

    events = sorted(
        ((c, t) for c in range(chunks) for t in range(steps)), key=lambda e: (2 * e[1] + e[0], -e[1])
    )
    ready = [i for i, (_, t) in enumerate(events) if t == steps - 1]
    each = -(-len(filler) // (ready[0] + 1))
    last = len(units) - 1
    done_u, relayed = [0], [0]

    def front():
        if done_u[0] == 0:
            err_load.wait()
            wait_all(turned_in, "turned", "turned")
        reduce_all(done_u[0])
        done_u[0] += 1

    for i, (c, t) in enumerate(events):
        for work in filler[:each]:
            work()
        filler = filler[each:]
        if i == len(events) - 1:
            relay(0)
            relayed[0] += 1
        gather_step(c, t)
        if t == 0 and c + 2 < chunks:
            launch(c + 2)
        if i > ready[0]:
            if t == steps - 1:
                front()
            if t < steps - 1 or c == chunks - 1:
                continue
        if t == steps - 1:
            prepare(done_u[0])
    behind = [0]

    def settle(tokens_beside=0):
        u = behind[0]
        for t in range(1, steps):
            advance(u, t)
        token_work(tokens_beside)
        if u >= LAG:
            finish(u - LAG)
        behind[0] += 1

    while done_u[0] <= last:
        ahead = done_u[0]
        prepare(ahead)
        front()
        if ahead < last and units[ahead + 1][0] and relayed[0] < chunks:
            relay(relayed[0])
            relayed[0] += 1
        while behind[0] <= ahead - AHEAD:
            settle()
    while behind[0] <= last:
        settle(3)
    token_work(len(token_tiles))
    for u in range(max(last + 1 - LAG, 0), last + 1):
        finish(u)

    pw_all[grp] = pw_acc[...].astype(BF16)
    for d in range(1, g):
        send(pw_all.at[grp], pw_all.at[grp], me, lax.rem(grp + d, g), "power", "power")
    wait_all(pw_all.at[0:g - 1], "power", "power")
    total = pw_all[0].astype(F32)
    for k in range(1, g):
        total += pw_all[k].astype(F32)
    power[0:rows, :] = total * (1.0 / g)

    lane = lax.broadcasted_iota(jnp.int32, (rank, LANES), 1)
    row = lax.broadcasted_iota(jnp.int32, (rank, LANES), 0)
    padded = power[...]
    gram = dot(padded.T, padded, HIGHEST)
    picked = gram[0:rank]
    for m in range(1, 3):
        picked = jnp.where(lane >= m * rank, gram[m * rank:(m + 1) * rank], picked)
    gram_all[me] = picked
    for d in range(1, n):
        send(gram_all.at[me], gram_all.at[me], lax.rem(me + d, n), grp, "gram", "gram")
    wait_all(gram_all.at[0:n - 1], "gram", "gram")
    picked = gram_all[0]
    for k in range(1, n):
        picked += gram_all[k]

    work = []
    for m in range(3):
        rolled = picked if m == 0 else pltpu.roll(picked, LANES - m * rank, 1)
        unit = jnp.where(lane == row + rank, 1.0, 0.0).astype(F32)
        work.append(jnp.where(lane < rank, rolled, unit))
    for j in range(rank):
        for m in range(3):
            a = work[m]
            inverse = 1.0 / jnp.sqrt(a[j:j + 1, j:j + 1])
            pivot_row = a[j:j + 1, :] * inverse
            column = a[:, j:j + 1] * inverse
            work[m] = jnp.where(row > j, a - column * pivot_row, jnp.where(row == j, pivot_row, a))
    for m in range(3):
        shift = ((m - 1) * rank) % LANES
        moved = work[m] if shift == 0 else pltpu.roll(work[m], shift, 1)
        inside_m = (lane >= m * rank) & (lane < (m + 1) * rank)
        block_diag[m * rank:(m + 1) * rank, :] = jnp.where(inside_m, moved, 0.0)
    hat_t = dot_nt(block_diag[...], power[...], HIGHEST)
    hat = dot_nt(power[0:rows, :], block_diag[...], HIGHEST)
    p_out[...] = hat_t[0:used, 0:rows]

    c_blocks = min(n, hidden // LANES)
    r_blocks = n // c_blocks
    c_size, r_size = hidden // c_blocks, used // r_blocks
    hat_top = hat_t.astype(BF16)
    hat_bottom = (hat_t - hat_top.astype(F32)).astype(BF16)
    for m in range(3):
        at = slice(m * rank, (m + 1) * rank)
        left = jnp.concatenate([hat_top[at], hat_bottom[at]], axis=0)
        both = dot(left, jnp.concatenate([high[m, j] for j in range(blocks)], axis=1))
        q_t[at, :] = both[0:rank] + both[rank:]
    spots = [
        (slice(c // c_blocks * r_size, (c // c_blocks + 1) * r_size),
         slice(c % c_blocks * c_size, (c % c_blocks + 1) * c_size))
        for c in range(n)
    ]
    for c in range(n):
        q_part[c] = q_t[spots[c]].astype(BF16)
    q_rs[me] = q_part[me]
    for d in range(1, n):
        to = lax.rem(me + d, n)
        send(q_part.at[to], q_rs.at[me], to, grp, "term", "term")
    wait_all(q_rs.at[0:n - 1], "term", "term")
    total = q_rs[0].astype(F32)
    for k in range(1, n):
        total += q_rs[k].astype(F32)
    q_grp[grp] = total.astype(BF16)
    for d in range(1, g):
        send(q_grp.at[grp], q_grp.at[grp], me, lax.rem(grp + d, g), "group", "group")
    wait_all(q_grp.at[0:g - 1], "group", "group")
    total = q_grp[0].astype(F32)
    for k in range(1, g):
        total += q_grp[k].astype(F32)
    q_all[me] = (total * (1.0 / g)).astype(BF16)
    for d in range(1, n):
        send(q_all.at[me], q_all.at[me], lax.rem(me + d, n), grp, "right", "right")
    wait_all(q_all.at[0:n - 1], "right", "right")
    for c in range(n):
        q_t[spots[c]] = q_all[c].astype(F32)
    q_out[...] = q_t[0:used, :]

    lanes = lax.broadcasted_iota(jnp.int32, (rows, LANES), 1)
    right = q_t[...].astype(BF16)
    right = jnp.concatenate([right, right], axis=0)
    for m in range(3):
        own = jnp.where((lanes >= m * rank) & (lanes < (m + 1) * rank), hat, 0.0)
        top = own.astype(BF16)
        left = jnp.concatenate([top, (own - top.astype(F32)).astype(BF16)], axis=1)
        for c in range(chunks):
            at = slice(c * wide, (c + 1) * wide)
            rebuilt = dot(left, right[:, at])
            merged = jnp.concatenate([
                high[m, j, 0:rows].astype(F32) + low[m, j, 0:rows].astype(F32)
                for j in (2 * c, 2 * c + 1)
            ], axis=1)
            err_out[:, m * hidden + c * wide:m * hidden + (c + 1) * wide] = (
                merged - rebuilt
            ).astype(BF16)
        at = pl.ds(m * hidden, hidden)
        local(err_out.at[:, at], new_err.at[0, :, at], chunks + 5)
    others = n // 2 - 1
    leave_refs["plane"] = (full.at[0:chunks, :, 0:others * rows, :], leave_refs["plane"][1])
    leave_refs["twin"] = (leave_refs["plane"][0], leave_refs["twin"][1])
    leave_refs["pair"] = (full.at[0:chunks], leave_refs["pair"][1])
    for t in range(steps):
        leave_refs["reduce", t] = (recv_bufs[t], leave_refs["reduce", t][1])
    leave_refs["hidden"] = (their_hid, leave_refs["hidden"][1])
    leave_refs["back"] = (their_back, leave_refs["back"][1])
    for leave, (ref, arrive) in leave_refs.items():
        whole(ref, arrive, leave).wait_send()
    pltpu.make_async_copy(tok_out, tok_grad, local_sems.at[chunks + 4]).wait()
    pltpu.make_async_copy(err_out, new_err.at[0], local_sems.at[chunks + 5]).wait()


def write_results(*refs):
    ins, outs, bufs, sems = refs[:4], refs[4:8], refs[8:12], refs[12]
    cuts = []
    for k in (0, 1, 2, 3):
        axis = len(ins[k].shape) - 2
        size = ins[k].shape[axis]
        count = 3 if k == 0 else 2 if k == 1 else 1
        for i in range(count):
            at = (slice(None),) * axis + (pl.ds(i * (size // count), size // count),)
            cuts.append((k, at))
    reads, writes = [], []
    for i, (k, at) in enumerate(cuts):
        reads.append(pltpu.make_async_copy(ins[k].at[at], bufs[k].at[at], sems.at[0, i]))
        reads[-1].start()
    for i, (k, at) in enumerate(cuts):
        reads[i].wait()
        writes.append(pltpu.make_async_copy(bufs[k].at[at], outs[k].at[at], sems.at[1, i]))
        writes[-1].start()
    for copy in writes:
        copy.wait()


def on_device(n, g, tokens, cotangent, gate_weight, up_weight, down_weight_t, error_memory, q_init):
    token_rows, depth = tokens.shape
    rows, hidden = gate_weight.shape
    rank = q_init.shape[2]
    used = 3 * rank
    bits = n.bit_length() - 1
    side = depth // 2
    wide = 2 * LANES
    chunks = hidden // wide
    blocks = hidden // LANES
    padded = -(-rows // LANES) * LANES
    q_rows = q_init.transpose(0, 2, 1).reshape(used, hidden)
    c_blocks = min(n, hidden // LANES)
    chunk = (used // (n // c_blocks), hidden // c_blocks)
    parts = 2 if rows % 32 == 0 else 1
    arrivals = (
        chunks * (bits - 1) * (parts + 1) + blocks + 2 * blocks * (bits - 1) + 2 * blocks + 6
    )
    leaves = 11 + bits - 1
    recv_shapes = [
        pltpu.VMEM((blocks * 3, 1 << (bits - 2 - t), rows, LANES), BF16) for t in range(bits - 1)
    ]
    vmem = pl.BlockSpec(memory_space=pltpu.VMEM)
    hbm = pl.BlockSpec(memory_space=pl.ANY)
    token_grad, new_error, hat_t, q_t = pl.pallas_call(
        functools.partial(kernel, n, g, rank),
        out_shape=(
            jax.ShapeDtypeStruct((token_rows, depth), BF16),
            jax.ShapeDtypeStruct((1, rows, 3 * hidden), BF16),
            jax.ShapeDtypeStruct((used, rows), F32),
            jax.ShapeDtypeStruct((used, hidden), F32),
        ),
        in_specs=[hbm] * 7,
        out_specs=(hbm, hbm, vmem, vmem),
        scratch_shapes=[
            pltpu.VMEM((2 * chunks, 3, depth, LANES), BF16),
            pltpu.VMEM((token_rows, depth), BF16),
            pltpu.VMEM((token_rows, depth), BF16),
            pltpu.VMEM((2, 2, side, token_rows), BF16),
            pltpu.VMEM((2, side, token_rows), BF16),
            pltpu.VMEM((token_rows, wide), F32),
            pltpu.VMEM((blocks, token_rows, LANES), BF16),
            pltpu.VMEM((blocks, token_rows, LANES), BF16),
            pltpu.VMEM((blocks, token_rows, wide), BF16),
            pltpu.VMEM((blocks, token_rows, wide), BF16),
            pltpu.VMEM((blocks, 3, side, LANES), BF16),
            *recv_shapes,
            pltpu.VMEM((3, blocks, padded, LANES), BF16),
            pltpu.VMEM((3, blocks, padded, LANES), BF16),
            pltpu.VMEM((3, hidden, wide), BF16),
            pltpu.VMEM((rows, 3 * hidden), BF16),
            pltpu.VMEM((LANES, hidden), F32),
            pltpu.VMEM((token_rows, depth), BF16),
            pltpu.VMEM((rows, 3 * hidden), BF16),
            pltpu.VMEM((rows, LANES), F32),
            pltpu.VMEM((padded, LANES), F32),
            pltpu.VMEM((LANES, LANES), F32),
            pltpu.VMEM((LANES, hidden), F32),
            pltpu.VMEM((g, rows, LANES), BF16),
            pltpu.VMEM((n, rank, LANES), F32),
            pltpu.VMEM((n,) + chunk, BF16),
            pltpu.VMEM((n,) + chunk, BF16),
            pltpu.VMEM((g,) + chunk, BF16),
            pltpu.VMEM((n,) + chunk, BF16),
            pltpu.SemaphoreType.DMA((leaves,)),
            pltpu.SemaphoreType.DMA((arrivals,)),
            pltpu.SemaphoreType.DMA((chunks + 6,)),
        ],
        compiler_params=pltpu.CompilerParams(
            collective_id=0, has_side_effects=True, vmem_limit_bytes=67_043_328
        ),
    )(tokens, cotangent, gate_weight, up_weight, down_weight_t, error_memory, q_rows)
    results = (token_grad, new_error, hat_t, q_t)
    token_grad, new_error, hat_t, q_t = pl.pallas_call(
        write_results,
        out_shape=tuple(jax.ShapeDtypeStruct(r.shape, r.dtype) for r in results),
        in_specs=[hbm] * 4,
        out_specs=(hbm,) * 4,
        scratch_shapes=[
            *(pltpu.VMEM(r.shape, r.dtype) for r in results),
            pltpu.SemaphoreType.DMA((2, 8)),
        ],
    )(*results)
    p_hat = hat_t.reshape(3, rank, rows).transpose(0, 2, 1)
    q_new = q_t.reshape(3, rank, hidden).transpose(0, 2, 1)
    return token_grad, new_error, p_hat, q_new


def solution(mesh):
    return jax.shard_map(
        functools.partial(on_device, mesh.shape["node"], mesh.shape["grp"]),
        mesh=mesh,
        in_specs=(
            P(("node", "grp"), None),
            P(("node", "grp"), None),
            P("node", None),
            P("node", None),
            P("node", None),
            P("grp", "node", None),
            P(),
        ),
        out_specs=(P(("node", "grp"), None), P("grp", "node", None), P(None, "node", None), P()),
        check_vma=False,
    )
```

time: 130 us -> 107 us (0.82)
  Pallas kernels: 124 us -> 106 us
  local copies, waits for them, and re-layouts: 5.09 us -> 0 us
    pallas_call x1, Pallas kernels: 124 us -> 103 us  [on_device(): pl.pallas_call(functools.partial(kernel, n, g, rank), out_shape=(jax.Shap...]
    unnamed x10 -> x0, local copies, waits for them, and re-layouts: 5.09 us -> none
    pallas_call x0 -> x1, Pallas kernels: none -> 2.89 us  [on_device(): pl.pallas_call(write_results, out_shape=tuple((jax.ShapeDtypeStruct(r.sha...]
where the time goes in v2:
time: 107 us
  Pallas kernels  106 us (99%)
    pallas_call x1, Pallas kernels, on_device(): pl.pallas_call(functools.partial(kernel, n, g, rank), out_shape=(jax.Shap...  103 us
    pallas_call x1, Pallas kernels, on_device(): pl.pallas_call(write_results, out_shape=tuple((jax.ShapeDtypeStruct(r.sha...  2.89 us

profile of v2, /device:TPU:0, one launch (start us, length us, event | category | flops | bytes accessed | tf_op | source)
XLA Modules:
  0.0 106.6 jit_solution(7538191469111650910)
XLA Ops:
  0.6 102.9 %shard_map.102 = (bf16[384,1792]{1,0:T(8,128)(2,1)}, bf16[1,224,3072]{2,1,0:T(8,128)(2,1)}, f32[96,224]{1,0:T(8,128)}, f32[96,1024]{1,0:T(8,128)}) custom-call(bf16[384,1792]{1,0:T(8,128)(2,1)} %tok_hbm.1, bf16[384,1792]{1,0:T(8,128)(2,1)} %cot_hbm.1, bf16[224,1024]{1,0:T(8,128)(2,1)} %w_gate.1, bf16[224,1024]{1,0:T(8,128)(2,1)} %w_up.1, ...), custom_call_target="tpu_custom_call" | custom-call | tf_op jit(solution)/shard_map/pallas_call | solution.py:564
  103.5 2.9 %shard_map.103 = (bf16[384,1792]{1,0:T(8,128)(2,1)}, bf16[1,224,3072]{2,1,0:T(8,128)(2,1)}, f32[96,224]{1,0:T(8,128)}, f32[96,1024]{1,0:T(8,128)}) custom-call(bf16[384,1792]{1,0:T(8,128)(2,1)} %get-tuple-element.12.refs_0_, bf16[1,224,3072]{2,1,0:T(8,128)(2,1)} %get-tuple-element.13.refs_1_, f32[96,224]{1,0:T(8,128)} %get-tuple-element.14.refs_2_, ...), custom_call_target="tpu_custom_call" | custom-call | tf_op jit(solution)/shard_map/pallas_call | solution.py:613

commit v3 on v2

--- a/solution.py
+++ b/solution.py
@@ -11,7 +11,7 @@
 MESH = pl.DeviceIdType.MESH
 F32, BF16 = jnp.float32, jnp.bfloat16
 HIGHEST = lax.Precision.HIGHEST
-AHEAD, LAG = 2, 2
+AHEAD, LAG, PIVOTS = 2, 4, 4
 LANES = 128
 
 
@@ -52,7 +52,7 @@
 ):
     bits = n.bit_length() - 1
     recv_bufs = rest[:bits - 1]
-    (high, low, q_right, err, q_rows, tok_out, err_out, pw_acc, power, block_diag, q_t, pw_all,
+    (high, low, q_right, err, q_rows, tok_out, err_out, hat_out, early, pw_acc, power, block_diag, q_t, pw_all,
      gram_all, q_part, q_rs, q_grp, q_all, send_sems, recv_sems, local_sems) = rest[bits - 1:]
     me, grp = lax.axis_index("node"), lax.axis_index("grp")
     rows, hidden = w_gate.shape
@@ -175,6 +175,7 @@
         launch(c)
 
     pw_acc[...] = jnp.zeros_like(pw_acc)
+    early[...] = jnp.zeros_like(early)
     power[...] = jnp.zeros_like(power)
     block_diag[...] = jnp.zeros_like(block_diag)
     q_t[...] = jnp.zeros_like(q_t)
@@ -208,6 +209,24 @@
                 q_right[m, at, 0:LANES] = jnp.where(inside_m, top.astype(F32), 0.0).astype(BF16)
                 q_right[m, at, LANES:] = jnp.where(inside_m, bottom.astype(F32), 0.0).astype(BF16)
 
+    units = [(0, c) for c in range(chunks)]
+    for c in range(chunks):
+        units.insert(min(chunks - 1 + 2 * c, len(units)), (1, c))
+    extra = len(units)
+    first_late = extra - (chunks - 1)
+
+    def memory_power():
+        err_load.wait()
+        for side_of, c in units[first_late:]:
+            j = column_block(side_of, c)
+            at = pl.ds(pl.multiple_of(j * LANES, LANES), LANES)
+            left = jnp.concatenate([
+                err[:, pl.ds(pl.multiple_of(m * hidden + j * LANES, LANES), LANES)]
+                for m in range(3)
+            ], axis=1)
+            both = dot(left, jnp.concatenate([q_right[m, at, :] for m in range(3)], axis=0))
+            pw_acc[...] += both[:, 0:LANES] + both[:, LANES:]
+
     filler = []
     for which, load in ((1, cot_load), (0, tok_load)):
         filler.append(load.wait)
@@ -215,7 +234,7 @@
             filler.append(functools.partial(turn, which, i))
         filler.append(functools.partial(
             send, turned.at[which, 1 - core], turned_in.at[which], pair, grp, "turned", "turned"))
-    filler.append(right_factors)
+    filler += [right_factors, memory_power]
 
     def forward(j):
         both = dot(tok[...], jnp.concatenate([full[j, 0], full[j, 1]], axis=1))
@@ -273,6 +292,8 @@
                     )
                     if t < steps - 1:
                         grads[u, m, at, :] = total.astype(BF16)
+                    elif u == extra:
+                        pw_acc[first:first + size] += total * scale
                     else:
                         span = pl.ds(pl.multiple_of(m * hidden + j * LANES, LANES), LANES)
                         memory = err[first:first + size, span].astype(F32)
@@ -284,7 +305,7 @@
     def reduce_finish(u, j, k):
         reduce_add(u, j, k, steps - 1)
         at = pl.ds(pl.multiple_of(j * LANES, LANES), LANES)
-        for m in group_m[k]:
+        for m in group_m[k] if u < first_late else ():
             both = dot(high[m, j, 0:rows], q_right[m, at, :])
             rest_part = dot(low[m, j, 0:rows], q_right[m, at, 0:LANES])
             pw_acc[...] += both[:, 0:LANES] + both[:, LANES:] + rest_part
@@ -306,9 +327,6 @@
         for _ in range(min(amount, len(token_tiles))):
             token_part(token_tiles.pop(0))
 
-    units = [(0, c) for c in range(chunks)]
-    for c in range(chunks):
-        units.insert(min(chunks - 1 + 2 * c, len(units)), (1, c))
 
     def prepare(u):
         side_of, c = units[u]
@@ -319,14 +337,26 @@
         backward(j)
         send(mine_back.at[j], their_back.at[j], pair, grp, ("back", u), "back")
 
-    def reduce_all(u):
+    def early_power(u, j, k):
+        at = pl.ds(pl.multiple_of(j * LANES, LANES), LANES)
+        right = jnp.concatenate([q_right[m, at, :] for m in group_m[k]], axis=0)
+        for i in range(2):
+            span = pl.ds(i * tile, tile)
+            left = jnp.concatenate([grads[u, m, span, :] for m in group_m[k]], axis=1)
+            both = dot(left, right)
+            early[span, :] += both[:, 0:LANES] + both[:, LANES:]
+
+    def reduce_all(u, sent):
         j = column_block(*units[u])
         wait_all(their_hid.at[j], ("hidden", u), "hidden")
-        gradient(u, j, 0)
-        reduce_start(u, 0, 0)
-        wait_all(their_back.at[j], ("back", u), "back")
-        gradient(u, j, 1)
-        reduce_start(u, 1, 0)
+        for k in range(2):
+            if k == 1:
+                wait_all(their_back.at[j], ("back", u), "back")
+            gradient(u, j, k)
+            if k in sent:
+                reduce_start(u, k, 0)
+            if u >= first_late:
+                early_power(u, j, k)
 
     def advance(u, t):
         j = column_block(*units[u])
@@ -347,11 +377,10 @@
     last = len(units) - 1
     done_u, relayed = [0], [0]
 
-    def front():
+    def front(sent=(0, 1)):
         if done_u[0] == 0:
-            err_load.wait()
             wait_all(turned_in, "turned", "turned")
-        reduce_all(done_u[0])
+        reduce_all(done_u[0], sent)
         done_u[0] += 1
 
     for i, (c, t) in enumerate(events):
@@ -373,11 +402,10 @@
             prepare(done_u[0])
     behind = [0]
 
-    def settle(tokens_beside=0):
+    def settle():
         u = behind[0]
         for t in range(1, steps):
             advance(u, t)
-        token_work(tokens_beside)
         if u >= LAG:
             finish(u - LAG)
         behind[0] += 1
@@ -385,26 +413,60 @@
     while done_u[0] <= last:
         ahead = done_u[0]
         prepare(ahead)
-        front()
+        front((0, 1) if ahead < last - 1 else (0,) if ahead < last else ())
         if ahead < last and units[ahead + 1][0] and relayed[0] < chunks:
             relay(relayed[0])
             relayed[0] += 1
-        while behind[0] <= ahead - AHEAD:
+        while ahead < last and behind[0] <= ahead - AHEAD:
             settle()
-    while behind[0] <= last:
-        settle(3)
-    token_work(len(token_tiles))
-    for u in range(max(last + 1 - LAG, 0), last + 1):
+    grads[extra, 2] = early[...].astype(BF16)
+    reduce_start(extra, 0, 0)
+    reduce_start(last - 1, 1, 0)
+    for u in range(max(behind[0] - LAG, 0), first_late):
         finish(u)
-
-    pw_all[grp] = pw_acc[...].astype(BF16)
+    for t in range(1, steps):
+        reduce_add(extra, 0, 0, t - 1)
+        reduce_start(extra, 0, t)
+    for u in range(behind[0], last - 1):
+        for t in range(1, steps):
+            advance(u, t)
+    for k in range(2):
+        reduce_start(last, k, 0)
+    reduce_add(extra, 0, 0, steps - 1)
+
+    packed = pw_all.shape[1] < rows
+    if packed:
+        head = pw_all.shape[1]
+        spare = lax.broadcasted_iota(jnp.int32, (head, LANES), 1) >= used
+        tail = pw_acc[head:, :]
+        moved = jnp.concatenate(
+            [pltpu.roll(tail, used - m * rank, 1) for m in range(3)], axis=0)
+        pw_all[grp] = jnp.where(spare, moved, pw_acc[0:head, :]).astype(BF16)
+    else:
+        pw_all[grp] = pw_acc[...].astype(BF16)
     for d in range(1, g):
         send(pw_all.at[grp], pw_all.at[grp], me, lax.rem(grp + d, g), "power", "power")
+    for t in range(1, steps):
+        advance(last - 1, t)
+    for u in range(first_late, last - 1):
+        finish(u)
+    token_work(len(token_tiles))
     wait_all(pw_all.at[0:g - 1], "power", "power")
     total = pw_all[0].astype(F32)
     for k in range(1, g):
         total += pw_all[k].astype(F32)
-    power[0:rows, :] = total * (1.0 / g)
+    total = total * (1.0 / g)
+    if packed:
+        short = rows - head
+        spot = lax.broadcasted_iota(jnp.int32, (short, LANES), 1) // rank
+        tail = jnp.zeros((short, LANES), F32)
+        for m in range(3):
+            back = pltpu.roll(total[m * short:(m + 1) * short], LANES - used + m * rank, 1)
+            tail = jnp.where(spot == m, back, tail)
+        power[0:head, :] = jnp.where(spare, 0.0, total)
+        power[head:rows, :] = tail
+    else:
+        power[0:rows, :] = total
 
     lane = lax.broadcasted_iota(jnp.int32, (rank, LANES), 1)
     row = lax.broadcasted_iota(jnp.int32, (rank, LANES), 0)
@@ -416,7 +478,11 @@
     gram_all[me] = picked
     for d in range(1, n):
         send(gram_all.at[me], gram_all.at[me], lax.rem(me + d, n), grp, "gram", "gram")
+    for t in range(1, steps):
+        advance(last, t)
+    finish(last - 1)
     wait_all(gram_all.at[0:n - 1], "gram", "gram")
+    finish(last)
     picked = gram_all[0]
     for k in range(1, n):
         picked += gram_all[k]
@@ -426,13 +492,30 @@
         rolled = picked if m == 0 else pltpu.roll(picked, LANES - m * rank, 1)
         unit = jnp.where(lane == row + rank, 1.0, 0.0).astype(F32)
         work.append(jnp.where(lane < rank, rolled, unit))
-    for j in range(rank):
+    for first in range(0, rank, PIVOTS):
         for m in range(3):
             a = work[m]
-            inverse = 1.0 / jnp.sqrt(a[j:j + 1, j:j + 1])
-            pivot_row = a[j:j + 1, :] * inverse
-            column = a[:, j:j + 1] * inverse
-            work[m] = jnp.where(row > j, a - column * pivot_row, jnp.where(row == j, pivot_row, a))
+            pivots = range(PIVOTS)
+            spread = [
+                jnp.broadcast_to(a[:, first + i:first + i + 1], (rank, LANES)) for i in pivots
+            ]
+            pivot_rows = [a[first + i:first + i + 1, :] for i in pivots]
+            update = None
+            for i in pivots:
+                inverse = 1.0 / spread[i][first + i:first + i + 1, :]
+                for k in range(i + 1, PIVOTS):
+                    factor = spread[i][first + k:first + k + 1, :] * inverse
+                    spread[k] -= spread[i] * factor
+                    pivot_rows[k] -= pivot_rows[i] * factor
+                term = spread[i] * (pivot_rows[i] * inverse)
+                update = term if update is None else update + term
+            a = jnp.where(row >= first + PIVOTS, a - update, a)
+            for i in pivots:
+                a = jnp.where(row == first + i, pivot_rows[i], a)
+            work[m] = a
+    for m in range(3):
+        diagonal = jnp.sum(jnp.where(lane == row, work[m], 0.0), axis=1, keepdims=True)
+        work[m] = work[m] * (1.0 / jnp.sqrt(diagonal))
     for m in range(3):
         shift = ((m - 1) * rank) % LANES
         moved = work[m] if shift == 0 else pltpu.roll(work[m], shift, 1)
@@ -440,7 +523,8 @@
         block_diag[m * rank:(m + 1) * rank, :] = jnp.where(inside_m, moved, 0.0)
     hat_t = dot_nt(block_diag[...], power[...], HIGHEST)
     hat = dot_nt(power[0:rows, :], block_diag[...], HIGHEST)
-    p_out[...] = hat_t[0:used, 0:rows]
+    hat_out[...] = hat_t[0:used, 0:rows]
+    local(hat_out, p_out, chunks + 6)
 
     c_blocks = min(n, hidden // LANES)
     r_blocks = n // c_blocks
@@ -480,7 +564,7 @@
     wait_all(q_all.at[0:n - 1], "right", "right")
     for c in range(n):
         q_t[spots[c]] = q_all[c].astype(F32)
-    q_out[...] = q_t[0:used, :]
+    local(q_t.at[0:used], q_out, chunks + 7)
 
     lanes = lax.broadcasted_iota(jnp.int32, (rows, LANES), 1)
     right = q_t[...].astype(BF16)
@@ -511,6 +595,8 @@
     leave_refs["back"] = (their_back, leave_refs["back"][1])
     for leave, (ref, arrive) in leave_refs.items():
         whole(ref, arrive, leave).wait_send()
+    pltpu.make_async_copy(hat_out, p_out, local_sems.at[chunks + 6]).wait()
+    pltpu.make_async_copy(q_t.at[0:used], q_out, local_sems.at[chunks + 7]).wait()
     pltpu.make_async_copy(tok_out, tok_grad, local_sems.at[chunks + 4]).wait()
     pltpu.make_async_copy(err_out, new_err.at[0], local_sems.at[chunks + 5]).wait()
 
@@ -551,15 +637,15 @@
     q_rows = q_init.transpose(0, 2, 1).reshape(used, hidden)
     c_blocks = min(n, hidden // LANES)
     chunk = (used // (n // c_blocks), hidden // c_blocks)
+    packed_rows = rows * 3 // 4 if rows % 32 == 0 and 4 * used == 3 * LANES else rows
     parts = 2 if rows % 32 == 0 else 1
     arrivals = (
-        chunks * (bits - 1) * (parts + 1) + blocks + 2 * blocks * (bits - 1) + 2 * blocks + 6
+        chunks * (bits - 1) * (parts + 1) + blocks + (2 * blocks + 1) * (bits - 1) + 2 * blocks + 6
     )
     leaves = 11 + bits - 1
     recv_shapes = [
-        pltpu.VMEM((blocks * 3, 1 << (bits - 2 - t), rows, LANES), BF16) for t in range(bits - 1)
+        pltpu.VMEM((blocks * 3 + 1, 1 << (bits - 2 - t), rows, LANES), BF16) for t in range(bits - 1)
     ]
-    vmem = pl.BlockSpec(memory_space=pltpu.VMEM)
     hbm = pl.BlockSpec(memory_space=pl.ANY)
     token_grad, new_error, hat_t, q_t = pl.pallas_call(
         functools.partial(kernel, n, g, rank),
@@ -570,7 +656,7 @@
             jax.ShapeDtypeStruct((used, hidden), F32),
         ),
         in_specs=[hbm] * 7,
-        out_specs=(hbm, hbm, vmem, vmem),
+        out_specs=(hbm,) * 4,
         scratch_shapes=[
             pltpu.VMEM((2 * chunks, 3, depth, LANES), BF16),
             pltpu.VMEM((token_rows, depth), BF16),
@@ -582,7 +668,7 @@
             pltpu.VMEM((blocks, token_rows, LANES), BF16),
             pltpu.VMEM((blocks, token_rows, wide), BF16),
             pltpu.VMEM((blocks, token_rows, wide), BF16),
-            pltpu.VMEM((blocks, 3, side, LANES), BF16),
+            pltpu.VMEM((blocks + 1, 3, side, LANES), BF16),
             *recv_shapes,
             pltpu.VMEM((3, blocks, padded, LANES), BF16),
             pltpu.VMEM((3, blocks, padded, LANES), BF16),
@@ -591,11 +677,13 @@
             pltpu.VMEM((LANES, hidden), F32),
             pltpu.VMEM((token_rows, depth), BF16),
             pltpu.VMEM((rows, 3 * hidden), BF16),
+            pltpu.VMEM((used, rows), F32),
+            pltpu.VMEM((side, LANES), F32),
             pltpu.VMEM((rows, LANES), F32),
             pltpu.VMEM((padded, LANES), F32),
             pltpu.VMEM((LANES, LANES), F32),
             pltpu.VMEM((LANES, hidden), F32),
-            pltpu.VMEM((g, rows, LANES), BF16),
+            pltpu.VMEM((g, packed_rows, LANES), BF16),
             pltpu.VMEM((n, rank, LANES), F32),
             pltpu.VMEM((n,) + chunk, BF16),
             pltpu.VMEM((n,) + chunk, BF16),
@@ -603,7 +691,7 @@
             pltpu.VMEM((n,) + chunk, BF16),
             pltpu.SemaphoreType.DMA((leaves,)),
             pltpu.SemaphoreType.DMA((arrivals,)),
-            pltpu.SemaphoreType.DMA((chunks + 6,)),
+            pltpu.SemaphoreType.DMA((chunks + 8,)),
         ],
         compiler_params=pltpu.CompilerParams(
             collective_id=0, has_side_effects=True, vmem_limit_bytes=67_043_328

time: 107 us -> 97.1 us (0.907)
  Pallas kernels: 106 us -> 96.1 us
    pallas_call x1, Pallas kernels: 103 us -> 93.2 us  [on_device(): pl.pallas_call(functools.partial(kernel, n, g, rank), out_shape=(jax.Shap...]
where the time goes in v3:
time: 97.1 us; the launch traced here: 96.9 us
  Pallas kernels  96.1 us (99%)
    pallas_call x1, Pallas kernels, on_device(): pl.pallas_call(functools.partial(kernel, n, g, rank), out_shape=(jax.Shap...  93.2 us
    pallas_call x1, Pallas kernels, on_device(): pl.pallas_call(write_results, out_shape=tuple((jax.ShapeDtypeStruct(r.sha...  2.89 us

profile of v3, /device:TPU:0, one launch (start us, length us, event | category | flops | bytes accessed | tf_op | source)
XLA Modules:
  0.0 96.9 jit_solution(18313283481269822657)
XLA Ops:
  0.6 93.2 %shard_map.102 = (bf16[384,1792]{1,0:T(8,128)(2,1)}, bf16[1,224,3072]{2,1,0:T(8,128)(2,1)}, f32[96,224]{1,0:T(8,128)}, f32[96,1024]{1,0:T(8,128)}) custom-call(bf16[384,1792]{1,0:T(8,128)(2,1)} %tok_hbm.1, bf16[384,1792]{1,0:T(8,128)(2,1)} %cot_hbm.1, bf16[224,1024]{1,0:T(8,128)(2,1)} %w_gate.1, bf16[224,1024]{1,0:T(8,128)(2,1)} %w_up.1, ...), custom_call_target="tpu_custom_call" | custom-call | tf_op jit(solution)/shard_map/pallas_call | solution.py:650
  93.9 2.9 %shard_map.103 = (bf16[384,1792]{1,0:T(8,128)(2,1)}, bf16[1,224,3072]{2,1,0:T(8,128)(2,1)}, f32[96,224]{1,0:T(8,128)}, f32[96,1024]{1,0:T(8,128)}) custom-call(bf16[384,1792]{1,0:T(8,128)(2,1)} %get-tuple-element.12.refs_0_, bf16[1,224,3072]{2,1,0:T(8,128)(2,1)} %get-tuple-element.13.refs_1_, f32[96,224]{1,0:T(8,128)} %get-tuple-element.14.refs_2_, ...), custom_call_target="tpu_custom_call" | custom-call | tf_op jit(solution)/shard_map/pallas_call | solution.py:701

commit v4 on v3

--- a/solution.py
+++ b/solution.py
@@ -122,13 +122,18 @@
         whole(ref, arrive, leave).wait_recv()
 
     if rows % 32 == 0:
-        parts = [[(0, rows // 2, 0), (rows // 2, rows // 2, 1)]] * chunks
+        row_parts = [[(0, rows // 2, 0), (rows // 2, rows // 2, 1)]] * chunks
     else:
-        parts = [[(0, rows, c % 2)] for c in range(chunks)]
+        row_parts = [[(0, rows, c % 2)] for c in range(chunks)]
+    parts = [
+        [part + cut for cut in (((0, 1), (1, 1), (2, 1)) if c == 0 else ((0, 3),)) for part in row_parts[c]]
+        for c in range(chunks)
+    ]
 
     def piece(j, mask, part):
         start = (me + offset(mask)) * rows + part[0]
-        return full.at[j, :, pl.ds(pl.multiple_of(start, math.gcd(rows, part[1])), part[1]), :]
+        at = pl.ds(pl.multiple_of(start, math.gcd(rows, part[1])), part[1])
+        return full.at[j, pl.ds(part[3], part[4]), at, :]
 
     def column_block(side_of, c):
         return 2 * c + (plane if side_of == 0 else 1 - plane)
@@ -144,7 +149,7 @@
 
     def gather_step(c, t):
         for part in parts[c]:
-            wait_all(full.at[2 * c, :, 0:part[1] << t, :], ("plane", c, t, part), "plane")
+            wait_all(full.at[2 * c, pl.ds(0, part[4]), 0:part[1] << t, :], ("plane", c, t, part), "plane")
             if t + 1 < steps:
                 gather_send(c, t + 1, part)
             for mask in new_masks(t, orders[part[2]]):
@@ -267,7 +272,7 @@
 
     def reduce_start(u, k, t):
         for m in group_m[k]:
-            for first, size, h in parts[u % chunks]:
+            for first, size, h in row_parts[u % chunks]:
                 bit = orders[h][t]
                 for slot, mask in enumerate(subsets(orders[h][t + 1:])):
                     at = half_node + half_flip[bit] + half_offset(mask)
@@ -282,7 +287,7 @@
         wait_all(
             recv_bufs[t].at[pl.ds(u * 3 + k, 1 + k)], ("reduce", u, k, t), ("reduce", t))
         for m in group_m[k]:
-            for first, size, h in parts[u % chunks]:
+            for first, size, h in row_parts[u % chunks]:
                 for slot, mask in enumerate(subsets(orders[h][t + 1:])):
                     at = (half_node + half_offset(mask)) * rows + first
                     at = pl.ds(pl.multiple_of(at, math.gcd(rows, size)), size)
@@ -337,26 +342,27 @@
         backward(j)
         send(mine_back.at[j], their_back.at[j], pair, grp, ("back", u), "back")
 
-    def early_power(u, j, k):
+    def early_power(u, j):
         at = pl.ds(pl.multiple_of(j * LANES, LANES), LANES)
-        right = jnp.concatenate([q_right[m, at, :] for m in group_m[k]], axis=0)
+        right = jnp.concatenate([q_right[m, at, :] for m in range(3)], axis=0)
         for i in range(2):
             span = pl.ds(i * tile, tile)
-            left = jnp.concatenate([grads[u, m, span, :] for m in group_m[k]], axis=1)
+            left = jnp.concatenate([grads[u, m, span, :] for m in range(3)], axis=1)
             both = dot(left, right)
             early[span, :] += both[:, 0:LANES] + both[:, LANES:]
 
-    def reduce_all(u, sent):
+    def reduce_all(u, sent, between):
         j = column_block(*units[u])
         wait_all(their_hid.at[j], ("hidden", u), "hidden")
         for k in range(2):
             if k == 1:
+                between()
                 wait_all(their_back.at[j], ("back", u), "back")
             gradient(u, j, k)
             if k in sent:
                 reduce_start(u, k, 0)
-            if u >= first_late:
-                early_power(u, j, k)
+        if u >= first_late:
+            early_power(u, j)
 
     def advance(u, t):
         j = column_block(*units[u])
@@ -377,10 +383,10 @@
     last = len(units) - 1
     done_u, relayed = [0], [0]
 
-    def front(sent=(0, 1)):
+    def front(sent=(0, 1), between=lambda: None):
         if done_u[0] == 0:
             wait_all(turned_in, "turned", "turned")
-        reduce_all(done_u[0], sent)
+        reduce_all(done_u[0], sent, between)
         done_u[0] += 1
 
     for i, (c, t) in enumerate(events):
@@ -410,28 +416,32 @@
             finish(u - LAG)
         behind[0] += 1
 
+    def relay_next(ahead):
+        if ahead < last and units[ahead + 1][0] and relayed[0] < chunks:
+            relay(relayed[0])
+            relayed[0] += 1
+
     while done_u[0] <= last:
         ahead = done_u[0]
         prepare(ahead)
-        front((0, 1) if ahead < last - 1 else (0,) if ahead < last else ())
-        if ahead < last and units[ahead + 1][0] and relayed[0] < chunks:
-            relay(relayed[0])
-            relayed[0] += 1
+        front((0, 1) if ahead < last - 1 else (), functools.partial(relay_next, ahead))
         while ahead < last and behind[0] <= ahead - AHEAD:
             settle()
     grads[extra, 2] = early[...].astype(BF16)
     reduce_start(extra, 0, 0)
-    reduce_start(last - 1, 1, 0)
+    reduce_start(last - 1, 0, 0)
     for u in range(max(behind[0] - LAG, 0), first_late):
         finish(u)
     for t in range(1, steps):
         reduce_add(extra, 0, 0, t - 1)
         reduce_start(extra, 0, t)
+    reduce_start(last - 1, 1, 0)
     for u in range(behind[0], last - 1):
         for t in range(1, steps):
             advance(u, t)
     for k in range(2):
         reduce_start(last, k, 0)
+    token_work(2)
     reduce_add(extra, 0, 0, steps - 1)
 
     packed = pw_all.shape[1] < rows
@@ -446,11 +456,7 @@
         pw_all[grp] = pw_acc[...].astype(BF16)
     for d in range(1, g):
         send(pw_all.at[grp], pw_all.at[grp], me, lax.rem(grp + d, g), "power", "power")
-    for t in range(1, steps):
-        advance(last - 1, t)
-    for u in range(first_late, last - 1):
-        finish(u)
-    token_work(len(token_tiles))
+    token_work(4)
     wait_all(pw_all.at[0:g - 1], "power", "power")
     total = pw_all[0].astype(F32)
     for k in range(1, g):
@@ -478,11 +484,13 @@
     gram_all[me] = picked
     for d in range(1, n):
         send(gram_all.at[me], gram_all.at[me], lax.rem(me + d, n), grp, "gram", "gram")
-    for t in range(1, steps):
-        advance(last, t)
-    finish(last - 1)
+    for u in (last - 1, last):
+        for t in range(1, steps):
+            advance(u, t)
+    for u in range(first_late, last - 1):
+        finish(u)
+    token_work(len(token_tiles))
     wait_all(gram_all.at[0:n - 1], "gram", "gram")
-    finish(last)
     picked = gram_all[0]
     for k in range(1, n):
         picked += gram_all[k]
@@ -531,22 +539,31 @@
     c_size, r_size = hidden // c_blocks, used // r_blocks
     hat_top = hat_t.astype(BF16)
     hat_bottom = (hat_t - hat_top.astype(F32)).astype(BF16)
-    for m in range(3):
-        at = slice(m * rank, (m + 1) * rank)
-        left = jnp.concatenate([hat_top[at], hat_bottom[at]], axis=0)
-        both = dot(left, jnp.concatenate([high[m, j] for j in range(blocks)], axis=1))
-        q_t[at, :] = both[0:rank] + both[rank:]
     spots = [
         (slice(c // c_blocks * r_size, (c // c_blocks + 1) * r_size),
          slice(c % c_blocks * c_size, (c % c_blocks + 1) * c_size))
         for c in range(n)
     ]
-    for c in range(n):
-        q_part[c] = q_t[spots[c]].astype(BF16)
+
+    def right_terms(first, end):
+        for m in range(3):
+            at = slice(m * rank, (m + 1) * rank)
+            left = jnp.concatenate([hat_top[at], hat_bottom[at]], axis=0)
+            both = dot(left, jnp.concatenate([high[m, j] for j in range(first, end)], axis=1))
+            q_t[at, first * LANES:end * LANES] = both[0:rank] + both[rank:]
+        for c in range(n):
+            if first * LANES <= spots[c][1].start and spots[c][1].stop <= end * LANES:
+                q_part[c] = q_t[spots[c]].astype(BF16)
+
+                @pl.when(me != c)
+                def _():
+                    send(q_part.at[c], q_rs.at[me], c, grp, "term", "term")
+
+    finish(last - 1)
+    right_terms(0, blocks - 2)
+    finish(last)
+    right_terms(blocks - 2, blocks)
     q_rs[me] = q_part[me]
-    for d in range(1, n):
-        to = lax.rem(me + d, n)
-        send(q_part.at[to], q_rs.at[me], to, grp, "term", "term")
     wait_all(q_rs.at[0:n - 1], "term", "term")
     total = q_rs[0].astype(F32)
     for k in range(1, n):
@@ -640,7 +657,7 @@
     packed_rows = rows * 3 // 4 if rows % 32 == 0 and 4 * used == 3 * LANES else rows
     parts = 2 if rows % 32 == 0 else 1
     arrivals = (
-        chunks * (bits - 1) * (parts + 1) + blocks + (2 * blocks + 1) * (bits - 1) + 2 * blocks + 6
+        (bits - 1) * (chunks * (parts + 1) + 2 * parts) + blocks + (2 * blocks + 1) * (bits - 1) + 2 * blocks + 6
     )
     leaves = 11 + bits - 1
     recv_shapes = [

time: 97.1 us -> 96.1 us (0.990)
  no operation moved by 1% of the time
where the time goes in v4:
time: 96.1 us; the launch traced here: 96 us
  Pallas kernels  95.2 us (99%)
    pallas_call x1, Pallas kernels, on_device(): pl.pallas_call(functools.partial(kernel, n, g, rank), out_shape=(jax.Shap...  92.3 us
    pallas_call x1, Pallas kernels, on_device(): pl.pallas_call(write_results, out_shape=tuple((jax.ShapeDtypeStruct(r.sha...  2.89 us

profile of v4, /device:TPU:0, one launch (start us, length us, event | category | flops | bytes accessed | tf_op | source)
XLA Modules:
  0.0 96.0 jit_solution(1330875408731505303)
XLA Ops:
  0.6 92.3 %shard_map.102 = (bf16[384,1792]{1,0:T(8,128)(2,1)}, bf16[1,224,3072]{2,1,0:T(8,128)(2,1)}, f32[96,224]{1,0:T(8,128)}, f32[96,1024]{1,0:T(8,128)}) custom-call(bf16[384,1792]{1,0:T(8,128)(2,1)} %tok_hbm.1, bf16[384,1792]{1,0:T(8,128)(2,1)} %cot_hbm.1, bf16[224,1024]{1,0:T(8,128)(2,1)} %w_gate.1, bf16[224,1024]{1,0:T(8,128)(2,1)} %w_up.1, ...), custom_call_target="tpu_custom_call" | custom-call | tf_op jit(solution)/shard_map/pallas_call | solution.py:667
  92.9 2.9 %shard_map.103 = (bf16[384,1792]{1,0:T(8,128)(2,1)}, bf16[1,224,3072]{2,1,0:T(8,128)(2,1)}, f32[96,224]{1,0:T(8,128)}, f32[96,1024]{1,0:T(8,128)}) custom-call(bf16[384,1792]{1,0:T(8,128)(2,1)} %get-tuple-element.12.refs_0_, bf16[1,224,3072]{2,1,0:T(8,128)(2,1)} %get-tuple-element.13.refs_1_, f32[96,224]{1,0:T(8,128)} %get-tuple-element.14.refs_2_, ...), custom_call_target="tpu_custom_call" | custom-call | tf_op jit(solution)/shard_map/pallas_call | solution.py:718
